TPU v7x, 32 devices: a whole 2x2x4 slice. The times are simulated.
32 devices in a mesh: rep: 2 (over y), pipe: 2 (over core), tp: 8 (over z, x).
Axes of the slice: x: 2, y: 2, z: 4, core: 2. Of those that a mesh axis runs over, the one named last changes fastest.
Arguments:
- hidden_entering: bfloat16 [2, 120, 8192], P('rep', None, 'tp'), parts along dimension 0, may hold values from -60 to 60
- segment_adapter: int32 [2, 3], P('rep'), parts along dimension 0, may hold values from 0 to 127, as said below
- segment_requests: int32 [2, 3], P('rep'), parts along dimension 0, may hold values from 10 to 40, as said below
- section_norm_gain: float32 [2, 8192], P('pipe'), may hold values from 0.25 to 1.75
- up_matrix: bfloat16 [2, 14336, 8192], P('pipe', 'tp'), may hold values from -0.0625 to 0.0625
- down_matrix: bfloat16 [2, 8192, 14336], P('pipe', 'tp'), may hold values from -0.046875 to 0.046875
- adapter_reduce: bfloat16 [2, 128, 131072], P('pipe', None, 'tp'), may hold values from -0.0625 to 0.0625
- adapter_expand: bfloat16 [2, 128, 229376], P('pipe', None, 'tp'), may hold values from -1.5 to 1.5
Outputs:
- section_out: bfloat16 [2, 2, 120, 8192], P('pipe', 'rep', None, 'tp'), parts along dimension 1
There are 2 independent parts, one for each index of `rep`. A program takes and returns all parts, laid end to end along the dimension named above; an argument that names none is the same for every part. Nothing has to cross between parts.
Inputs may be any that keep to these rules, and one draw needn't show every extreme that they name: `segment_adapter`: within each micro-batch the adapter ids of its segments do not decrease. The first segment_requests[m, j] rows of segment j of micro-batch m hold requests; the other rows are padding.
All inputs are finite; a program needn't handle non-finite values.
Results may differ from a plain program's by a relative error of at most 0.0045.
Values may be sent and summed in bfloat16 or wider, within the bound.
A program may use at most 128 MiB of HBM per device.

v0:
```python
import functools

import jax
import jax.numpy as jnp
from jax import lax
from jax.experimental import pallas as pl
from jax.experimental.pallas import tpu as pltpu
from jax.sharding import PartitionSpec as P

EPSILON = 1e-05


def shifted(x, axis, by):
    size = lax.axis_size(axis)
    pairs = [(i, i + by) for i in range(size) if 0 <= i + by < size]
    return lax.ppermute(x, axis, pairs)


def times_rows(left, weight):
    return lax.dot_general(
        left, weight, (((1,), (1,)), ((), ())), preferred_element_type=jnp.float32
    )


def block_step(
    current, unit_ids, unit_live, gain_full, up_weight, down_weight, shrink_weight, expand_weight
):
    row_count = current.shape[0]
    col_count = current.shape[1]
    hid_count = up_weight.shape[0]
    segments = unit_ids.shape[0]
    seg_rows = row_count // segments
    feature_width = gain_full.shape[0]
    adapter_rank_count = shrink_weight.shape[1] // col_count
    column = lax.axis_index("tp") * col_count
    gain_mine = lax.dynamic_slice_in_dim(gain_full, column, col_count, 0)
    widened_local = current.astype(jnp.float32)
    local_scaled = (widened_local * gain_mine).astype(jnp.bfloat16)
    input_panel = shrink_weight[unit_ids].reshape(segments, col_count, adapter_rank_count)
    output_panel = expand_weight[unit_ids].reshape(segments, hid_count, adapter_rank_count)
    partial_value = jnp.einsum(
        "sdr,spd->rsp",
        input_panel,
        local_scaled.reshape(segments, seg_rows, col_count),
        preferred_element_type=jnp.float32,
    ).reshape(adapter_rank_count, row_count)
    local_squares = jnp.sum(widened_local * widened_local, axis=1)
    reduced, squares = lax.psum((partial_value, local_squares), "tp")
    widened = lax.all_gather(current, "tp", axis=1, tiled=True).astype(jnp.float32)
    scaled = (widened * gain_full).astype(jnp.bfloat16)
    up_total = times_rows(scaled, up_weight)
    inverse = lax.rsqrt(squares / feature_width + EPSILON)
    low_rank = (
        (reduced * inverse[None, :])
        .astype(jnp.bfloat16)
        .reshape(adapter_rank_count, segments, seg_rows)
    )
    adapted = jnp.einsum(
        "rsp,sdr->spd", low_rank, output_panel, preferred_element_type=jnp.float32
    ).reshape(row_count, hid_count)
    up_sum = inverse[:, None] * up_total + adapted
    hidden_act = jax.nn.silu(up_sum).astype(jnp.bfloat16)
    down_sum = times_rows(lax.all_gather(hidden_act, "tp", axis=1, tiled=True), down_weight)
    updated = (widened_local + down_sum).astype(jnp.bfloat16)
    positions = lax.broadcasted_iota(jnp.int32, (segments, seg_rows), 1)
    row_kept = (positions < unit_live[:, None]).reshape(row_count, 1)
    return jnp.where(row_kept, updated, jnp.zeros_like(updated))


MESH = pl.DeviceIdType.MESH
PIECE = 256
COLUMNS = 2
VMEM_BYTES = 67_043_328


def section_kernel(
    live_ref, x_ref, gain_ref, reduce_ref, expand_ref, up_hbm, down_hbm, out_ref,
    up_v, down_v, xs, act, current, acc, partial,
    up_sem, down_sem, part_send, part_recv, x_send, x_recv, a_send, a_recv, pipe_sem,
):
    shards, x_pieces, rows, _ = xs.shape
    a_pieces = act.shape[1]
    cols = x_ref.shape[1]
    hidden = up_v.shape[0]
    width = shards * cols
    segments = reduce_ref.shape[0]
    rank = reduce_ref.shape[1]
    seg_rows = rows // segments
    depth = shards // COLUMNS
    me = lax.axis_index("tp")
    stage = lax.axis_index("pipe")
    stages = lax.axis_size("pipe")
    z, x = me // COLUMNS, me % COLUMNS
    partner = z * COLUMNS + (1 - x)

    def up_copy(c):
        span = pl.ds(c * PIECE, PIECE)
        return pltpu.make_async_copy(up_hbm.at[span, :], up_v.at[span, :], up_sem.at[c])

    def down_copy(t):
        span = pl.ds(pl.multiple_of(t * hidden, 128), hidden)
        return pltpu.make_async_copy(down_hbm.at[:, span], down_v.at[:, span], down_sem.at[t])

    @pl.loop(0, a_pieces)
    def _(c):
        up_copy(c).start()

    @pl.loop(0, shards)
    def _(i):
        down_copy((me + i) % shards).start()

    barrier = pltpu.get_barrier_semaphore()

    @pl.loop(1, shards)
    def _(i):
        pl.semaphore_signal(barrier, inc=1, device_id={"tp": (me + i) % shards}, device_id_type=MESH)

    @pl.when(stage > 0)
    def _():
        pl.semaphore_signal(barrier, inc=1, device_id={"pipe": stage - 1}, device_id_type=MESH)

    @pl.when(stage < stages - 1)
    def _():
        pl.semaphore_signal(barrier, inc=1, device_id={"pipe": stage + 1}, device_id_type=MESH)

    neighbours = jnp.where(stage > 0, 1, 0) + jnp.where(stage < stages - 1, 1, 0)
    pl.semaphore_wait(barrier, shards - 1 + neighbours)

    def hand_over():
        return pltpu.make_async_remote_copy(
            src_ref=out_ref, dst_ref=current, send_sem=pipe_sem.at[0], recv_sem=pipe_sem.at[1],
            device_id={"pipe": (stage + 1) % stages}, device_id_type=MESH)

    @pl.when(stage == 0)
    def _():
        current[...] = x_ref[...]

    @pl.when(stage > 0)
    def _():
        hand_over().wait_recv()

    class Spread:
        def __init__(self, buf, send, recv, pieces):
            self.buf, self.send, self.recv, self.pieces = buf, send, recv, pieces

        def copy(self, t, c, way, target):
            return pltpu.make_async_remote_copy(
                src_ref=self.buf.at[t, c], dst_ref=self.buf.at[t, c],
                send_sem=self.send.at[way, t, c], recv_sem=self.recv.at[t, c],
                device_id={"tp": target}, device_id_type=MESH)

        def each(self, source_z, column, c, do):
            t = source_z * COLUMNS + column
            own, first = column == x, c == 0
            along = jnp.logical_or(own, first)
            across = jnp.logical_and(own, jnp.logical_or(c != 0, source_z == z))

            @pl.when(jnp.logical_and(along, jnp.logical_and(source_z <= z, z < depth - 1)))
            def _():
                do(self.copy(t, c, 0, (me + COLUMNS) % shards))

            @pl.when(jnp.logical_and(along, jnp.logical_and(source_z >= z, z > 0)))
            def _():
                do(self.copy(t, c, 1, (me + shards - COLUMNS) % shards))

            @pl.when(across)
            def _():
                do(self.copy(t, c, 2, partner))

        def forward(self, source_z, column, c):
            self.each(source_z, column, c, lambda d: d.start())

        def arrive(self, t, c):
            self.copy(t, c, 2, partner).wait_recv()

        def pass_on(self, source_z, column, c):
            @pl.when(jnp.logical_and(source_z >= 0, source_z < depth))
            def _():
                self.arrive(source_z * COLUMNS + column, c)
                self.forward(source_z, column, c)

        def relay(self, step, column, c):
            for source_z in (z - step, z + step) if step else (z,):
                self.pass_on(source_z, column, c)

        def partner_arrive(self, t):
            @pl.loop(1, self.pieces)
            def _(c):
                self.arrive(t, c)

        def drain(self):
            @pl.loop(0, depth)
            def _(source_z):
                @pl.loop(0, self.pieces)
                def _(c):
                    self.each(source_z, x, c, lambda d: d.wait_send())

                self.each(source_z, 1 - x, 0, lambda d: d.wait_send())

    x_side = Spread(xs, x_send, x_recv, x_pieces)
    a_side = Spread(act, a_send, a_recv, a_pieces)

    for c in range(x_pieces):
        gain = gain_ref[:, pl.ds(pl.multiple_of(me * cols + c * PIECE, 128), PIECE)]
        wide = current[:, c * PIECE:(c + 1) * PIECE].astype(jnp.float32)
        xs[me, c] = (wide * gain).astype(jnp.bfloat16)
        x_side.forward(z, x, c)

    lane_seg = lax.broadcasted_iota(jnp.int32, (1, 128), 1) // seg_rows
    nt = (((1,), (1,)), ((), ()))
    total = jnp.zeros((segments * rank, 128), jnp.float32)
    squares = jnp.zeros((8, 128), jnp.float32)
    lane_pad = 128 - rows
    for c in range(x_pieces):
        span = slice(c * PIECE, (c + 1) * PIECE)
        mine = jnp.concatenate([xs[me, c], jnp.zeros((lane_pad, PIECE), jnp.bfloat16)], axis=0) if lane_pad else xs[me, c]
        panel = reduce_ref[:, :, span].reshape(segments * rank, PIECE)
        total += lax.dot_general(panel, mine, nt, preferred_element_type=jnp.float32)
        wide = current[:, span].astype(jnp.float32)
        square = wide * wide
        if lane_pad:
            square = jnp.concatenate([square, jnp.zeros((lane_pad, PIECE), jnp.float32)], axis=0)
        squares += lax.dot_general(jnp.ones((8, PIECE), jnp.float32), square, nt,
                                   precision=lax.Precision.HIGHEST, preferred_element_type=jnp.float32)
    picked = jnp.zeros((rank, 128), jnp.float32)
    for s in range(segments):
        picked += jnp.where(lane_seg == s, total[s * rank:(s + 1) * rank], 0.0)
    partial[me, 0:rank] = picked
    partial[me, rank:rank + 8] = squares

    def part_copy(owner, target):
        return pltpu.make_async_remote_copy(
            src_ref=partial.at[owner], dst_ref=partial.at[owner], send_sem=part_send.at[target],
            recv_sem=part_recv.at[owner], device_id={"tp": target}, device_id_type=MESH)

    @pl.loop(1, shards)
    def _(i):
        part_copy(me, (me + i) % shards).start()

    x_side.relay(0, 1 - x, 0)
    for step in range(1, depth):
        @pl.loop(0, x_pieces)
        def _(c):
            x_side.relay(step, x, c)

        x_side.relay(step, 1 - x, 0)

    @pl.loop(1, shards)
    def _(i):
        owner = (me + i) % shards
        part_copy(owner, owner).wait_recv()

    summed = partial[0]
    for t in range(1, shards):
        summed = summed + partial[t]
    inverse_lane = lax.rsqrt(summed[rank:rank + 1] / width + EPSILON)
    low_lane = (summed[0:rank] * inverse_lane).astype(jnp.bfloat16).astype(jnp.float32)
    blocks = [jnp.where(lane_seg == s, low_lane, 0.0) for s in range(segments)]
    blocks.append(jnp.broadcast_to(inverse_lane, (8, 128)))
    blocks.append(jnp.zeros((128 - segments * rank - 8, 128), jnp.float32))
    turned = jnp.transpose(jnp.concatenate(blocks, axis=0))[:rows]
    low_rank = turned[:, :segments * rank].astype(jnp.bfloat16)
    inverse = turned[:, segments * rank:segments * rank + 1]

    @pl.loop(0, depth)
    def _(source_z):
        x_side.partner_arrive(source_z * COLUMNS + (1 - x))

    LAG = 3

    def relays(k):
        for step in range(1, depth):
            c = k - LAG * step

            @pl.when(jnp.logical_and(c >= 0, c < a_pieces))
            def _():
                a_side.relay(step, x, c)

        for step in range(depth):
            @pl.when(k == LAG * (step + 1))
            def _():
                a_side.relay(step, 1 - x, 0)

    @pl.loop(0, a_pieces)
    def _(k):
        up_copy(k).wait()
        span = pl.ds(pl.multiple_of(k * PIECE, PIECE), PIECE)
        base = jnp.zeros((rows, PIECE), jnp.float32)
        for t in range(shards):
            for c in range(x_pieces):
                at = t * cols + c * PIECE
                base += lax.dot_general(xs[t, c], up_v[span, at:at + PIECE], nt, preferred_element_type=jnp.float32)
        panel = expand_ref[:, :, span].reshape(segments * rank, PIECE)
        adapted = jnp.dot(low_rank, panel, preferred_element_type=jnp.float32)
        value = inverse * base + adapted
        act[me, k] = (value / (1.0 + jnp.exp(-value))).astype(jnp.bfloat16)
        a_side.forward(z, x, k)
        relays(k)

    acc[...] = current[...].astype(jnp.float32)

    def down_part(t):
        down_copy(t).wait()

        @pl.loop(0, cols // PIECE)
        def _(n):
            block = pl.ds(pl.multiple_of(n * PIECE, PIECE), PIECE)
            part = acc[:, block]
            for c in range(a_pieces):
                span = pl.ds(pl.multiple_of(t * hidden + c * PIECE, 128), PIECE)
                part += lax.dot_general(act[t, c], down_v[block, span], nt, preferred_element_type=jnp.float32)
            acc[:, block] = part

    def down_at(z_of, column):
        @pl.when(jnp.logical_and(z_of >= 0, z_of < depth))
        def _():
            t = z_of * COLUMNS + column

            @pl.when(column != x)
            def _():
                a_side.partner_arrive(t)

            down_part(t)

    order = [[(0, 0)], [(0, 1)], [(1, 0)], [(-1, 0)], [(1, 1), (-1, 1)], [(2, 0), (-2, 0)], [(2, 1), (-2, 1)], [], []]
    begun = [item for items in order for item in items]
    rest = [(d * sign, o) for d in range(1, depth) for o in (0, 1) for sign in (1, -1)]
    ticks = LAG * (depth - 1)
    order += [[item for item in rest if item not in begun]]
    for j in range(max(ticks, len(order))):
        if j < ticks:
            relays(a_pieces + j)
        for far, other in order[j] if j < len(order) else ():
            down_at(z + far, (x + other) % COLUMNS)

    row = lax.broadcasted_iota(jnp.int32, (rows, 1), 0)
    kept = row < 0
    for s in range(segments):
        low = s * seg_rows
        kept = jnp.logical_or(kept, jnp.logical_and(row >= low, row < low + jnp.minimum(live_ref[s], seg_rows)))
    out_ref[...] = jnp.where(kept, acc[...], 0.0).astype(jnp.bfloat16)

    @pl.when(stage < stages - 1)
    def _():
        copy = hand_over()
        copy.start()
        copy.wait_send()

    @pl.loop(1, shards)
    def _(i):
        part_copy(me, (me + i) % shards).wait_send()

    x_side.drain()
    a_side.drain()


def fused_sections(current, ids, live, gain, up_weight, down_weight, shrink_weight, expand_weight):
    rows, cols = current.shape
    hidden = up_weight.shape[0]
    segments = ids.shape[0]
    shards = lax.axis_size("tp")
    rank = shrink_weight.shape[1] // cols

    def panels(table, length):
        picked = [lax.dynamic_slice_in_dim(table, ids[s], 1, 0) for s in range(segments)]
        return jnp.concatenate(picked, axis=0).reshape(segments, length, rank).transpose(0, 2, 1)

    x_pieces, a_pieces = cols // PIECE, hidden // PIECE
    vmem = pl.BlockSpec(memory_space=pltpu.VMEM)
    hbm = pl.BlockSpec(memory_space=pl.ANY)
    dma = pltpu.SemaphoreType.DMA
    return pl.pallas_call(
        section_kernel,
        out_shape=jax.ShapeDtypeStruct((rows, cols), jnp.bfloat16),
        in_specs=[pl.BlockSpec(memory_space=pltpu.SMEM)] + [vmem] * 4 + [hbm] * 2,
        out_specs=vmem,
        scratch_shapes=[
            pltpu.VMEM(up_weight.shape, jnp.bfloat16),
            pltpu.VMEM(down_weight.shape, jnp.bfloat16),
            pltpu.VMEM((shards, x_pieces, rows, PIECE), jnp.bfloat16),
            pltpu.VMEM((shards, a_pieces, rows, PIECE), jnp.bfloat16),
            pltpu.VMEM((rows, cols), jnp.bfloat16),
            pltpu.VMEM((rows, cols), jnp.float32),
            pltpu.VMEM((shards, rank + 8, 128), jnp.float32),
            dma((a_pieces,)), dma((shards,)),
            dma((shards,)), dma((shards,)),
            dma((3, shards, x_pieces)), dma((shards, x_pieces)),
            dma((3, shards, a_pieces)), dma((shards, a_pieces)),
            dma((2,)),
        ],
        compiler_params=pltpu.CompilerParams(
            collective_id=0, has_side_effects=True, vmem_limit_bytes=VMEM_BYTES
        ),
    )(live, current, gain[None, :], panels(shrink_weight, cols), panels(expand_weight, hidden),
      up_weight, down_weight)


def run_window(
    units, unit_ids, unit_live, gain_full, up_weight, down_weight, shrink_weight, expand_weight
):
    section_index = lax.axis_index("pipe")
    sections = lax.axis_size("pipe")
    unit_count = units.shape[0]
    tick_total = unit_count + sections - 1

    def process(tick_index, received, collected):
        position = jnp.clip(tick_index - section_index, 0, unit_count - 1)
        arriving = lax.dynamic_index_in_dim(
            units, jnp.minimum(tick_index, unit_count - 1), 0, keepdims=False
        )
        current = jnp.where(section_index == 0, arriving, received)
        ids_here = lax.dynamic_index_in_dim(unit_ids, position, 0, keepdims=False)
        live_here = lax.dynamic_index_in_dim(unit_live, position, 0, keepdims=False)
        produced = block_step(
            current,
            ids_here,
            live_here,
            gain_full,
            up_weight,
            down_weight,
            shrink_weight,
            expand_weight,
        )
        lag = tick_index - section_index
        in_window = jnp.logical_and(lag >= 0, lag < unit_count)
        placed = lax.dynamic_update_index_in_dim(collected, produced, position, 0)
        return (produced, jnp.where(in_window, placed, collected))

    def one_tick(tick_index, state):
        produced, collected = process(tick_index, state[0], state[1])
        return (shifted(produced, "pipe", 1), collected)

    start_state = (jnp.zeros_like(units[0]), jnp.zeros_like(units))
    received, collected = lax.fori_loop(0, tick_total - 1, one_tick, start_state)
    produced, collected = process(tick_total - 1, received, collected)
    return collected


def per_device(
    hidden_entering,
    segment_adapter,
    segment_requests,
    section_norm_gain,
    up_matrix,
    down_matrix,
    adapter_reduce,
    adapter_expand,
):
    batch_list = hidden_entering.shape[0]
    row_count = hidden_entering.shape[1]
    col_count = hidden_entering.shape[2]
    hidden = up_matrix.shape[1]
    fits = 2 * hidden * col_count * 2 * lax.axis_size("tp") < VMEM_BYTES - 7 * 2**20
    whole_pieces = col_count % PIECE == 0 and hidden % PIECE == 0 and hidden >= 4 * PIECE
    if batch_list == 1 and whole_pieces and fits and row_count <= 128:
        produced = fused_sections(
            hidden_entering[0],
            segment_adapter[0],
            segment_requests[0],
            section_norm_gain[0],
            up_matrix[0],
            down_matrix[0],
            adapter_reduce[0],
            adapter_expand[0],
        )
        return produced.reshape(1, batch_list, row_count, col_count)
    collected = run_window(
        hidden_entering,
        segment_adapter,
        segment_requests,
        section_norm_gain[0],
        up_matrix[0],
        down_matrix[0],
        adapter_reduce[0],
        adapter_expand[0],
    )
    return collected.reshape(1, batch_list, row_count, col_count)


def solution(mesh):
    return jax.shard_map(
        per_device,
        mesh=mesh,
        in_specs=(
            P("rep", None, "tp"),
            P("rep", None),
            P("rep", None),
            P("pipe", None),
            P("pipe", "tp", None),
            P("pipe", "tp", None),
            P("pipe", None, "tp"),
            P("pipe", None, "tp"),
        ),
        out_specs=P("pipe", "rep", None, "tp"),
        check_vma=False,
    )
```

profile of v0, /device:TPU:1, one launch (start us, length us, event | category | flops | bytes accessed | tf_op | source)
XLA Modules:
  0.0 120.4 jit_solution(7777597147645322204)
XLA Ops:
  0.0 1.4 %fusion = (s32[1,1]{1,0:T(1,128)}, s32[1,1]{1,0:T(1,128)}, s32[1,1]{1,0:T(1,128)}) fusion(s32[1,3]{1,0:T(1,128)} %param.9), kind=kLoop, calls=%fused_computation.8 | loop fusion | bytes 24 | tf_op jit(solution)/shard_map/slice | solution.py:365
  7.0 2.3 %dynamic-slice_reduce_fusion.2 = (bf16[28672]{0:T(1024)(128)(2,1)S(1)}, bf16[28672]{0:T(1024)(128)(2,1)S(1)}, bf16[28672]{0:T(1024)(128)(2,1)S(1)}) fusion(bf16[1,128,28672]{2,1,0:T(8,128)(2,1)} %param.15, s32[]{:T(128)S(6)} %select_n.12, s32[]{:T(128)S(6)} %select_n.14, s32[]{:T(128)S(6)} %select_n.13), kind=kLoop, calls=%fused_computation.3 | loop fusion | bytes 344076 | tf_op jit(solution)/shard_map/dynamic_slice | solution.py:365
  9.4 0.3 concatenate.24
  9.7 0.2 copy.12
  9.9 0.3 concatenate.25
  10.2 0.2 copy.13
  10.4 0.3 concatenate.26
  10.8 0.2 copy.14
  10.9 0.7 maximum_bitcast_fusion.expand_ref
  11.6 1.7 %dynamic-slice_reduce_fusion.5 = (bf16[16384]{0:T(1024)(128)(2,1)S(1)}, bf16[16384]{0:T(1024)(128)(2,1)S(1)}, bf16[16384]{0:T(1024)(128)(2,1)S(1)}) fusion(bf16[1,128,16384]{2,1,0:T(8,128)(2,1)} %param.14, s32[]{:T(128)S(6)} %select_n.12, s32[]{:T(128)S(6)} %select_n.14, s32[]{:T(128)S(6)} %select_n.13), kind=kLoop, calls=%fused_computation.7 | loop fusion | bytes 196620 | tf_op jit(solution)/shard_map/dynamic_slice | solution.py:365
  13.3 0.2 concatenate.21
  13.6 0.1 copy.10
  13.7 0.2 concatenate.22
  13.9 0.1 copy.11
  14.0 0.2 concatenate.20
  14.2 0.1 copy.9
  14.3 0.7 maximum_bitcast_fusion.1.reduce_ref
  15.0 103.8 %shard_map.82 = bf16[120,1024]{1,0:T(8,128)(2,1)} custom-call(s32[3]{0:T(128)} %bitcast.16, bf16[120,1024]{1,0:T(8,128)(2,1)} %bitcast.15, f32[1,8192]{1,0:T(1,128)} %gain_ref.1, bf16[3,16,1024]{2,1,0:T(8,128)(2,1)} %maximum_bitcast_fusion.1.reduce_ref, bf16[3,16,1792]{2,1,0:T(8,128)(2,1)} %maximum_bitcast_fusion.expand_ref, bf16[1792,8192]{1,0:T(8,128)(2,1)} %bitcast.12, ...), custom_call_target="tpu_custom_call" | custom-call | tf_op jit(solution)/shard_map/pallas_call | solution.py:372
  118.8 1.7 %copy.16 = bf16[1,1,120,1024]{3,2,1,0:T(8,128)(2,1)} copy(bf16[1,1,120,1024]{3,2,1,0:T(8,128)(2,1)} %bitcast.14) | data formatting | bytes 491520
where the time goes:
time: 121 us; the launch traced here: 120 us
  Pallas kernels  104 us (86%)
  local copies, waits for them, and re-layouts  9.52 us (8%)
  between operations  5.76 us (5%)
  other arithmetic  1.36 us (1%)
    pallas_call x1, Pallas kernels, fused_sections(): pl.pallas_call(section_kernel, out_shape=jax.ShapeDtypeStruct((rows, cols...  104 us
    dynamic_slice x2, local copies, waits for them, and re-layouts, panels(): lax.dynamic_slice_in_dim(table, ids[s], 1, 0)  4.04 us
    concatenate x12, local copies, waits for them, and re-layouts, panels(): jnp.concatenate(picked, axis=0).reshape(segments, length, rank)  2.47 us

commit v1 on v0

v1 whole, which is shorter than its diff:
```python
import functools

import jax
import jax.numpy as jnp
from jax import lax
from jax.experimental import pallas as pl
from jax.experimental.pallas import tpu as pltpu
from jax.sharding import PartitionSpec as P

EPSILON = 1e-05


def shifted(x, axis, by):
    size = lax.axis_size(axis)
    pairs = [(i, i + by) for i in range(size) if 0 <= i + by < size]
    return lax.ppermute(x, axis, pairs)


def times_rows(left, weight):
    return lax.dot_general(
        left, weight, (((1,), (1,)), ((), ())), preferred_element_type=jnp.float32
    )


def block_step(
    current, unit_ids, unit_live, gain_full, up_weight, down_weight, shrink_weight, expand_weight
):
    row_count = current.shape[0]
    col_count = current.shape[1]
    hid_count = up_weight.shape[0]
    segments = unit_ids.shape[0]
    seg_rows = row_count // segments
    feature_width = gain_full.shape[0]
    adapter_rank_count = shrink_weight.shape[1] // col_count
    column = lax.axis_index("tp") * col_count
    gain_mine = lax.dynamic_slice_in_dim(gain_full, column, col_count, 0)
    widened_local = current.astype(jnp.float32)
    local_scaled = (widened_local * gain_mine).astype(jnp.bfloat16)
    input_panel = shrink_weight[unit_ids].reshape(segments, col_count, adapter_rank_count)
    output_panel = expand_weight[unit_ids].reshape(segments, hid_count, adapter_rank_count)
    partial_value = jnp.einsum(
        "sdr,spd->rsp",
        input_panel,
        local_scaled.reshape(segments, seg_rows, col_count),
        preferred_element_type=jnp.float32,
    ).reshape(adapter_rank_count, row_count)
    local_squares = jnp.sum(widened_local * widened_local, axis=1)
    reduced, squares = lax.psum((partial_value, local_squares), "tp")
    widened = lax.all_gather(current, "tp", axis=1, tiled=True).astype(jnp.float32)
    scaled = (widened * gain_full).astype(jnp.bfloat16)
    up_total = times_rows(scaled, up_weight)
    inverse = lax.rsqrt(squares / feature_width + EPSILON)
    low_rank = (
        (reduced * inverse[None, :])
        .astype(jnp.bfloat16)
        .reshape(adapter_rank_count, segments, seg_rows)
    )
    adapted = jnp.einsum(
        "rsp,sdr->spd", low_rank, output_panel, preferred_element_type=jnp.float32
    ).reshape(row_count, hid_count)
    up_sum = inverse[:, None] * up_total + adapted
    hidden_act = jax.nn.silu(up_sum).astype(jnp.bfloat16)
    down_sum = times_rows(lax.all_gather(hidden_act, "tp", axis=1, tiled=True), down_weight)
    updated = (widened_local + down_sum).astype(jnp.bfloat16)
    positions = lax.broadcasted_iota(jnp.int32, (segments, seg_rows), 1)
    row_kept = (positions < unit_live[:, None]).reshape(row_count, 1)
    return jnp.where(row_kept, updated, jnp.zeros_like(updated))


MESH = pl.DeviceIdType.MESH
PIECE = 256
COLUMNS = 2
LANES = 128
VMEM_BYTES = 67_043_328
NT = (((1,), (1,)), ((), ()))


class Spread:
    def __init__(self, buf, send, recv, pieces, z, x, depth, starts_own):
        self.buf, self.send, self.recv, self.pieces = buf, send, recv, pieces
        self.z, self.x, self.depth, self.starts_own = z, x, depth, starts_own
        self.shards = depth * COLUMNS
        self.me = z * COLUMNS + x

    def copy(self, t, c, way, target):
        return pltpu.make_async_remote_copy(
            src_ref=self.buf.at[t, c], dst_ref=self.buf.at[t, c],
            send_sem=self.send.at[way, t, c], recv_sem=self.recv.at[t, c],
            device_id={"tp": target}, device_id_type=MESH)

    def each(self, source_z, column, c, do):
        z, x, me = self.z, self.x, self.me
        t = source_z * COLUMNS + column
        own, special = column == x, c == self.pieces - 1
        along = jnp.logical_or(own, special)
        across = jnp.logical_and(own, jnp.logical_or(c != self.pieces - 1, source_z == z))

        @pl.when(jnp.logical_and(along, jnp.logical_and(source_z <= z, z < self.depth - 1)))
        def _():
            do(self.copy(t, c, 0, (me + COLUMNS) % self.shards))

        @pl.when(jnp.logical_and(along, jnp.logical_and(source_z >= z, z > 0)))
        def _():
            do(self.copy(t, c, 1, (me + self.shards - COLUMNS) % self.shards))

        @pl.when(across)
        def _():
            do(self.copy(t, c, 2, z * COLUMNS + (1 - x)))

    def forward(self, source_z, column, c):
        self.each(source_z, column, c, lambda d: d.start())

    def arrive(self, t, c):
        self.copy(t, c, 2, self.z * COLUMNS + (1 - self.x)).wait_recv()

    def relay(self, step, column, c):
        for source_z in (self.z - step, self.z + step) if step else (self.z,):
            @pl.when(jnp.logical_and(source_z >= 0, source_z < self.depth))
            def _():
                self.arrive(source_z * COLUMNS + column, c)
                self.forward(source_z, column, c)

    def drain(self):
        @pl.loop(0, self.depth)
        def _(source_z):
            @pl.when(jnp.logical_or(source_z != self.z, self.starts_own))
            def _():
                @pl.loop(0, self.pieces)
                def _(c):
                    self.each(source_z, self.x, c, lambda d: d.wait_send())

            self.each(source_z, 1 - self.x, self.pieces - 1, lambda d: d.wait_send())


def section_kernel(
    ids_ref, live_ref, gain_ref, x_hbm, reduce_hbm, expand_hbm, up_hbm, down_hbm, out_ref,
    up_v, down_v, xs, act, acc, sq, shrink, expand, partial,
    up_sem, down_sem, tab_sem, own_sem, part_send, part_recv, x_send, x_recv, a_send, a_recv, h_send,
):
    shards, x_pieces, rows, _ = xs.shape
    a_pieces = act.shape[1]
    cols = x_pieces * PIECE
    hidden = up_v.shape[0]
    width = shards * cols
    adapters, shrink_len = reduce_hbm.shape
    expand_len = expand_hbm.shape[1]
    segments = ids_ref.shape[0]
    rank = shrink_len // cols
    table_width = shards * hidden // (PIECE * rank) * (PIECE * rank)
    seg_rows = rows // segments
    depth = shards // COLUMNS
    me = lax.axis_index("tp")
    stage = lax.axis_index("pipe")
    stages = lax.axis_size("pipe")
    z, x = me // COLUMNS, me % COLUMNS
    partner = z * COLUMNS + (1 - x)
    upper = (me + COLUMNS) % shards
    lower = (me + shards - COLUMNS) % shards
    f32, bf16 = jnp.float32, jnp.bfloat16

    few = jnp.minimum(z, depth - 1 - z)
    layer = [z]
    for i in range(1, depth):
        both = i <= 2 * few
        far = jnp.where(both, (i + 1) // 2, i - few)
        down_side = jnp.where(both, i % 2 == 1, z > depth - 1 - z)
        layer.append(jnp.where(down_side, z - far, z + far))

    def shard(i, other):
        return layer[i] * COLUMNS + ((1 - x) if other else x)

    visits = [shard(i, other) for i in range(depth) for other in (False, True)]

    def up_copy(t):
        span = pl.ds(pl.multiple_of(t * cols, LANES), cols)
        return pltpu.make_async_copy(up_hbm.at[:, span], up_v.at[:, span], up_sem.at[t])

    def down_copy(t):
        span = pl.ds(pl.multiple_of(t * hidden, LANES), hidden)
        return pltpu.make_async_copy(down_hbm.at[:, span], down_v.at[:, span], down_sem.at[t])

    def own_copy(c):
        return pltpu.make_async_copy(x_hbm.at[:, c * PIECE:(c + 1) * PIECE], xs.at[me, c], own_sem.at[c])

    tables = []
    for table, length in ((reduce_hbm, shrink_len), (expand_hbm, expand_len)):
        blocks = []
        for at in range(0, length, table_width):
            size = min(table_width, length - at)
            k = sum(len(t) for t in tables) + len(blocks)
            copy = pltpu.make_async_copy(
                table.at[:, at:at + size],
                down_v.at[k * adapters:(k + 1) * adapters, 0:size], tab_sem.at[k])
            blocks.append((k, size, copy))
        tables.append(blocks)

    @pl.when(stage == 0)
    def _():
        for c in range(x_pieces):
            own_copy(c).start()

    up_copy(me).start()
    for blocks in tables:
        for _k, _size, copy in blocks:
            copy.start()
    for t in visits[1:]:
        up_copy(t).start()

    barrier = pltpu.get_barrier_semaphore()

    @pl.loop(1, shards)
    def _(i):
        pl.semaphore_signal(barrier, inc=1, device_id={"tp": (me + i) % shards}, device_id_type=MESH)

    def greet(target):
        pl.semaphore_signal(
            barrier, inc=1, device_id={"pipe": stage - 1, "tp": target}, device_id_type=MESH)

    @pl.when(stage > 0)
    def _():
        greet(me)
        greet(partner)

        @pl.when(z < depth - 1)
        def _():
            greet(upper)

        @pl.when(z > 0)
        def _():
            greet(lower)

    fed = 2 + jnp.where(z < depth - 1, 1, 0) + jnp.where(z > 0, 1, 0)
    pl.semaphore_wait(barrier, shards - 1 + jnp.where(stage < stages - 1, fed, 0))

    x_side = Spread(xs, x_send, x_recv, x_pieces, z, x, depth, stage == 0)
    a_side = Spread(act, a_send, a_recv, a_pieces, z, x, depth, stage >= 0)

    def hand_over(c, way, target):
        return pltpu.make_async_remote_copy(
            src_ref=out_ref.at[c], dst_ref=xs.at[me, c],
            send_sem=h_send.at[way, c], recv_sem=x_recv.at[me, c],
            device_id={"pipe": (stage + 1) % stages, "tp": target}, device_id_type=MESH)

    def hand_each(c, do):
        @pl.when(stage < stages - 1)
        def _():
            @pl.when(z < depth - 1)
            def _():
                do(hand_over(c, 0, upper))

            @pl.when(z > 0)
            def _():
                do(hand_over(c, 1, lower))

            do(hand_over(c, 2, partner))
            do(hand_over(c, 3, me))

    @pl.when(stage == 0)
    def _():
        for c in range(x_pieces):
            own_copy(c).wait()
            x_side.forward(z, x, c)

    row_seg = lax.broadcasted_iota(jnp.int32, (rows, LANES), 0) // seg_rows
    lane_group = lax.broadcasted_iota(jnp.int32, (rows, LANES), 1) // rank
    in_segment = row_seg == lane_group

    picks = jnp.zeros((8 * segments, adapters), f32)
    pick_row = lax.broadcasted_iota(jnp.int32, picks.shape, 0)
    pick_col = lax.broadcasted_iota(jnp.int32, picks.shape, 1)
    for s in range(segments):
        hit = jnp.logical_and(pick_row // 8 == s, pick_col == ids_ref[s])
        picks = jnp.where(hit, 1.0, picks)
    picks = picks.astype(bf16)
    flat = PIECE * rank
    lane_tiles = flat // LANES
    spot_row = lax.broadcasted_iota(jnp.int32, (PIECE, LANES), 0) % 8
    spot_lane = lax.broadcasted_iota(jnp.int32, (PIECE, LANES), 1) // rank
    spot = spot_row == spot_lane
    fold_row = lax.broadcasted_iota(jnp.int32, (segments * LANES, LANES), 0)
    fold_col = lax.broadcasted_iota(jnp.int32, (segments * LANES, LANES), 1)
    fold = jnp.where(fold_col == fold_row // LANES * rank + fold_row % rank, 1.0, 0.0).astype(bf16)

    for blocks in tables:
        for _k, _size, copy in blocks:
            copy.wait()
    for blocks, dest in zip(tables, (shrink, expand)):
        done = 0
        for k, size, copy in blocks:
            first = done

            @pl.loop(0, size // flat)
            def _(j):
                span = pl.ds(pl.multiple_of(j * flat, LANES), flat)
                table = down_v[k * adapters:(k + 1) * adapters, span]
                got = jnp.dot(picks, table, preferred_element_type=f32)
                parts = []
                for s in range(segments):
                    tall = jnp.concatenate(
                        [got[8 * s:8 * s + 8, LANES * i:LANES * (i + 1)] for i in range(lane_tiles)], axis=0)
                    parts.append(jnp.where(spot, tall, 0.0).astype(bf16))
                panel = jnp.dot(jnp.concatenate(parts, axis=1), fold, preferred_element_type=f32)
                at = pl.multiple_of((first + j) * PIECE, PIECE)
                dest[pl.ds(at, PIECE), :] = panel.astype(bf16)

            done += size // flat

    for t in visits:
        down_copy(t).start()

    def raw(t, c):
        return xs[t, c].astype(f32)

    def scaled(t, c, wide):
        at = pl.multiple_of(t * cols + c * PIECE, LANES)
        return (wide * gain_ref[:, pl.ds(at, PIECE)]).astype(bf16)

    def squares(wide):
        square = wide * wide
        return square[:, :LANES] + square[:, LANES:]

    def up_tile(n, t, c):
        at = pl.multiple_of(t * cols + c * PIECE, LANES)
        return up_v[n * PIECE:(n + 1) * PIECE, pl.ds(at, PIECE)]

    def up_add(items, init):
        lefts = []
        total = jnp.zeros((rows, LANES), f32) if init else sq[...]
        for t, c in items:
            wide = raw(t, c)
            total += squares(wide)
            lefts.append(scaled(t, c, wide))
        sq[...] = total
        for n in range(a_pieces):
            block = slice(n * PIECE, (n + 1) * PIECE)
            part = jnp.zeros((rows, PIECE), f32)
            for (t, c), left in zip(items, lefts):
                part += lax.dot_general(left, up_tile(n, t, c), NT, preferred_element_type=f32)
            acc[:, block] = part if init else acc[:, block] + part

    @pl.when(stage > 0)
    def _():
        for c in range(x_pieces):
            x_side.arrive(me, c)

    up_copy(me).wait()
    up_add([(me, c) for c in range(x_pieces)], True)

    def part_copy(owner, target):
        return pltpu.make_async_remote_copy(
            src_ref=partial.at[owner], dst_ref=partial.at[owner], send_sem=part_send.at[target],
            recv_sem=part_recv.at[owner], device_id={"tp": target}, device_id_type=MESH)

    low = jnp.zeros((rows, LANES), f32)
    for c in range(x_pieces):
        low += jnp.dot(scaled(me, c, raw(me, c)), shrink[c * PIECE:(c + 1) * PIECE, :],
                       preferred_element_type=f32)
    low = jnp.where(in_segment, low, 0.0)
    if rows < LANES:
        low = jnp.concatenate([low, jnp.zeros((LANES - rows, LANES), f32)], axis=0)
    turned = jnp.transpose(low)
    picked = turned[0:rank]
    for s in range(1, segments):
        picked = picked + turned[s * rank:(s + 1) * rank]
    partial[me] = picked

    @pl.loop(1, shards)
    def _(i):
        part_copy(me, (me + i) % shards).start()

    def spread_in(side, step, weights, pieces_of, add):
        for t in weights:
            t.wait()

        @pl.loop(0, side.pieces)
        def _(c):
            side.relay(step, x, c)

            @pl.when(c < side.pieces - 1)
            def _():
                side.arrive(shard(step - 1, True), c)

            @pl.when(c == side.pieces - 1)
            def _():
                side.relay(step - 1, 1 - x, c)

            add([(t, c) for t in pieces_of])

    for i in range(1, depth):
        fresh = [shard(i - 1, True), shard(i, False)]
        spread_in(x_side, i, [up_copy(t) for t in fresh], fresh, lambda items: up_add(items, False))

    last = shard(depth - 1, True)
    up_copy(last).wait()

    @pl.loop(0, x_pieces - 2)
    def _(c):
        x_side.arrive(last, c)
        up_add([(last, c)], False)

    @pl.loop(1, shards)
    def _(i):
        owner = (me + i) % shards
        part_copy(owner, owner).wait_recv()

    summed = partial[0]
    for t in range(1, shards):
        summed = summed + partial[t]
    stacked = jnp.concatenate([summed] * segments + [jnp.zeros((LANES - segments * rank, LANES), f32)], axis=0)
    low = jnp.where(in_segment, jnp.transpose(stacked)[:rows], 0.0)

    x_side.arrive(last, x_pieces - 2)
    x_side.relay(depth - 1, 1 - x, x_pieces - 1)
    finals = [(last, x_pieces - 2), (last, x_pieces - 1)]
    square = sq[...]
    lefts = []
    for t, c in finals:
        wide = raw(t, c)
        square += squares(wide)
        lefts.append(scaled(t, c, wide))
    inverse = lax.rsqrt(jnp.sum(square, axis=1, keepdims=True) / width + EPSILON)
    low_rank = (low * inverse).astype(bf16)

    for n in range(a_pieces):
        block = slice(n * PIECE, (n + 1) * PIECE)
        base = jnp.zeros((rows, PIECE), f32)
        for (t, c), left in zip(finals, lefts):
            base += lax.dot_general(left, up_tile(n, t, c), NT, preferred_element_type=f32)
        adapted = lax.dot_general(low_rank, expand[block, :], NT, preferred_element_type=f32)
        value = inverse * (acc[:, block] + base) + adapted
        act[me, n] = (value / (1.0 + jnp.exp(-value))).astype(bf16)
        a_side.forward(z, x, n)

    def down_tile(n, t, c):
        at = pl.multiple_of(t * hidden + c * PIECE, LANES)
        return down_v[n * PIECE:(n + 1) * PIECE, pl.ds(at, PIECE)]

    def down_add(items):
        for n in range(x_pieces):
            block = slice(n * PIECE, (n + 1) * PIECE)
            part = jnp.zeros((rows, PIECE), f32)
            for t, c in items:
                part += lax.dot_general(act[t, c], down_tile(n, t, c), NT, preferred_element_type=f32)
            acc[:, block] = acc[:, block] + part

    for n in range(x_pieces):
        acc[:, n * PIECE:(n + 1) * PIECE] = xs[me, n].astype(f32)

    down_copy(me).wait()
    for i in range(1, depth):
        fresh = [shard(i - 1, True), shard(i, False)]
        spread_in(a_side, i, [down_copy(t) for t in fresh],
                  ([me] if i == 1 else []) + fresh, down_add)

    down_copy(last).wait()

    @pl.loop(0, a_pieces - 2)
    def _(c):
        a_side.arrive(last, c)
        down_add([(last, c)])

    row = lax.broadcasted_iota(jnp.int32, (rows, 1), 0)
    kept = row < 0
    for s in range(segments):
        start = s * seg_rows
        kept = jnp.logical_or(kept, jnp.logical_and(row >= start, row < start + jnp.minimum(live_ref[s], seg_rows)))

    a_side.arrive(last, a_pieces - 2)
    a_side.relay(depth - 1, 1 - x, a_pieces - 1)
    for n in range(x_pieces):
        block = slice(n * PIECE, (n + 1) * PIECE)
        part = jnp.zeros((rows, PIECE), f32)
        for c in (a_pieces - 2, a_pieces - 1):
            part += lax.dot_general(act[last, c], down_tile(n, last, c), NT, preferred_element_type=f32)
        out_ref[n] = jnp.where(kept, acc[:, block] + part, 0.0).astype(bf16)
        hand_each(n, lambda d: d.start())

    @pl.loop(0, x_pieces)
    def _(c):
        hand_each(c, lambda d: d.wait_send())

    @pl.loop(1, shards)
    def _(i):
        part_copy(me, (me + i) % shards).wait_send()

    x_side.drain()
    a_side.drain()


def fused_sections(current, ids, live, gain, up_weight, down_weight, shrink_weight, expand_weight):
    rows, cols = current.shape
    hidden = up_weight.shape[0]
    shards = lax.axis_size("tp")
    rank = shrink_weight.shape[1] // cols
    x_pieces, a_pieces = cols // PIECE, hidden // PIECE
    vmem = pl.BlockSpec(memory_space=pltpu.VMEM)
    smem = pl.BlockSpec(memory_space=pltpu.SMEM)
    hbm = pl.BlockSpec(memory_space=pl.ANY)
    dma = pltpu.SemaphoreType.DMA
    flat = PIECE * rank
    blocks = table_blocks(shards * hidden // flat * flat, shrink_weight, expand_weight)
    pieces = pl.pallas_call(
        section_kernel,
        out_shape=jax.ShapeDtypeStruct((x_pieces, rows, PIECE), jnp.bfloat16),
        in_specs=[smem, smem, vmem] + [hbm] * 5,
        out_specs=vmem,
        scratch_shapes=[
            pltpu.VMEM(up_weight.shape, jnp.bfloat16),
            pltpu.VMEM(down_weight.shape, jnp.bfloat16),
            pltpu.VMEM((shards, x_pieces, rows, PIECE), jnp.bfloat16),
            pltpu.VMEM((shards, a_pieces, rows, PIECE), jnp.bfloat16),
            pltpu.VMEM((rows, hidden), jnp.float32),
            pltpu.VMEM((rows, LANES), jnp.float32),
            pltpu.VMEM((cols, LANES), jnp.bfloat16),
            pltpu.VMEM((hidden, LANES), jnp.bfloat16),
            pltpu.VMEM((shards, rank, LANES), jnp.float32),
            dma((shards,)), dma((shards,)), dma((blocks,)), dma((x_pieces,)),
            dma((shards,)), dma((shards,)),
            dma((3, shards, x_pieces)), dma((shards, x_pieces)),
            dma((3, shards, a_pieces)), dma((shards, a_pieces)),
            dma((4, x_pieces)),
        ],
        compiler_params=pltpu.CompilerParams(
            collective_id=0, has_side_effects=True, vmem_limit_bytes=VMEM_BYTES
        ),
    )(ids, live, gain[None, :], current, shrink_weight, expand_weight, up_weight, down_weight)
    return pieces.transpose(1, 0, 2).reshape(rows, cols)


def table_blocks(width, *tables):
    return sum(-(-table.shape[1] // width) for table in tables)


def kernel_fits(row_count, col_count, hidden, segments, shrink_weight, expand_weight):
    shards = lax.axis_size("tp")
    adapters, flat_cols = shrink_weight.shape
    rank = flat_cols // col_count
    flat = PIECE * rank
    width = shards * hidden // flat * flat
    if col_count % PIECE or hidden % PIECE or hidden < 4 * PIECE or col_count < 4 * PIECE:
        return False
    if row_count > LANES or rank * 8 != LANES or segments * rank > LANES or adapters % LANES:
        return False
    if shards % COLUMNS or shards < 2 * COLUMNS or col_count > hidden:
        return False
    if not width or table_blocks(width, shrink_weight, expand_weight) * adapters > col_count:
        return False
    return 2 * hidden * col_count * 2 * shards < VMEM_BYTES - 7 * 2**20


def run_window(
    units, unit_ids, unit_live, gain_full, up_weight, down_weight, shrink_weight, expand_weight
):
    section_index = lax.axis_index("pipe")
    sections = lax.axis_size("pipe")
    unit_count = units.shape[0]
    tick_total = unit_count + sections - 1

    def process(tick_index, received, collected):
        position = jnp.clip(tick_index - section_index, 0, unit_count - 1)
        arriving = lax.dynamic_index_in_dim(
            units, jnp.minimum(tick_index, unit_count - 1), 0, keepdims=False
        )
        current = jnp.where(section_index == 0, arriving, received)
        ids_here = lax.dynamic_index_in_dim(unit_ids, position, 0, keepdims=False)
        live_here = lax.dynamic_index_in_dim(unit_live, position, 0, keepdims=False)
        produced = block_step(
            current,
            ids_here,
            live_here,
            gain_full,
            up_weight,
            down_weight,
            shrink_weight,
            expand_weight,
        )
        lag = tick_index - section_index
        in_window = jnp.logical_and(lag >= 0, lag < unit_count)
        placed = lax.dynamic_update_index_in_dim(collected, produced, position, 0)
        return (produced, jnp.where(in_window, placed, collected))

    def one_tick(tick_index, state):
        produced, collected = process(tick_index, state[0], state[1])
        return (shifted(produced, "pipe", 1), collected)

    start_state = (jnp.zeros_like(units[0]), jnp.zeros_like(units))
    received, collected = lax.fori_loop(0, tick_total - 1, one_tick, start_state)
    produced, collected = process(tick_total - 1, received, collected)
    return collected


def per_device(
    hidden_entering,
    segment_adapter,
    segment_requests,
    section_norm_gain,
    up_matrix,
    down_matrix,
    adapter_reduce,
    adapter_expand,
):
    batch_list = hidden_entering.shape[0]
    row_count = hidden_entering.shape[1]
    col_count = hidden_entering.shape[2]
    hidden = up_matrix.shape[1]
    segments = segment_adapter.shape[1]
    if batch_list == 1 and kernel_fits(
        row_count, col_count, hidden, segments, adapter_reduce[0], adapter_expand[0]
    ):
        produced = fused_sections(
            hidden_entering[0],
            segment_adapter[0],
            segment_requests[0],
            section_norm_gain[0],
            up_matrix[0],
            down_matrix[0],
            adapter_reduce[0],
            adapter_expand[0],
        )
        return produced.reshape(1, batch_list, row_count, col_count)
    collected = run_window(
        hidden_entering,
        segment_adapter,
        segment_requests,
        section_norm_gain[0],
        up_matrix[0],
        down_matrix[0],
        adapter_reduce[0],
        adapter_expand[0],
    )
    return collected.reshape(1, batch_list, row_count, col_count)


def solution(mesh):
    return jax.shard_map(
        per_device,
        mesh=mesh,
        in_specs=(
            P("rep", None, "tp"),
            P("rep", None),
            P("rep", None),
            P("pipe", None),
            P("pipe", "tp", None),
            P("pipe", "tp", None),
            P("pipe", None, "tp"),
            P("pipe", None, "tp"),
        ),
        out_specs=P("pipe", "rep", None, "tp"),
        check_vma=False,
    )
```

time: 121 us -> 99.5 us (0.82)
  local copies, waits for them, and re-layouts: 9.52 us -> 1.89 us
  Pallas kernels: 104 us -> 97.3 us
  between operations: 5.76 us -> 0.01 us
  other arithmetic: 1.36 us -> 0 us
    pallas_call x1, Pallas kernels: 104 us -> 97.3 us  [fused_sections(): pl.pallas_call(section_kernel, out_shape=jax.ShapeDtypeStruct((x_pieces,...]
    dynamic_slice x2 -> x0, local copies, waits for them, and re-layouts: 4.04 us -> none  [panels(): lax.dynamic_slice_in_dim(table, ids[s], 1, 0)]
    concatenate x12 -> x0, local copies, waits for them, and re-layouts: 2.47 us -> none  [panels(): jnp.concatenate(picked, axis=0).reshape(segments, length, rank)]
    unnamed x1 -> x0, local copies, waits for them, and re-layouts: 1.65 us -> none
    transpose x2 -> x0, other arithmetic: 1.36 us -> none  [panels(): jnp.concatenate(picked, axis=0).reshape(segments, length, rank)]
    slice x1 -> x0, local copies, waits for them, and re-layouts: 1.36 us -> none  [panels(): ids[s]]
where the time goes in v1:
time: 99.5 us; the launch traced here: 99.2 us
  Pallas kernels  97.3 us (98%)
  local copies, waits for them, and re-layouts  1.89 us (2%)
    pallas_call x1, Pallas kernels, fused_sections(): pl.pallas_call(section_kernel, out_shape=jax.ShapeDtypeStruct((x_pieces,...  97.3 us

profile of v1, /device:TPU:1, one launch (start us, length us, event | category | flops | bytes accessed | tf_op | source)
XLA Modules:
  0.0 99.2 jit_solution(14364707022823282004)
XLA Ops:
  0.0 97.3 %shard_map.82 = bf16[4,120,256]{2,1,0:T(8,128)(2,1)} custom-call(s32[3]{0:T(128)} %bitcast.14, s32[3]{0:T(128)} %bitcast.15, f32[1,8192]{1,0:T(1,128)} %gain_ref.1, bf16[120,1024]{1,0:T(8,128)(2,1)} %bitcast.13, bf16[128,16384]{1,0:T(8,128)(2,1)} %bitcast.11, bf16[128,28672]{1,0:T(8,128)(2,1)} %bitcast.10, bf16[1792,8192]{1,0:T(8,128)(2,1)} %bitcast.8, ...), custom_call_target="tpu_custom_call" | custom-call | tf_op jit(solution)/shard_map/pallas_call | solution.py:502
  97.4 1.0 %copy.9 = bf16[120,4,256]{2,1,0:T(4,128)(2,1)S(1)} copy(bf16[120,4,256]{2,0,1:T(8,128)(2,1)} %bitcast.12) | data formatting | bytes 491520 | tf_op jit(solution)/shard_map/transpose | solution.py:527
  98.4 0.9 reshape_reshape.3

commit v2 on v1

--- a/solution.py
+++ b/solution.py
@@ -194,17 +194,25 @@
             blocks.append((k, size, copy))
         tables.append(blocks)
 
+    def start_tables(blocks):
+        for _k, _size, copy in blocks:
+            copy.start()
+
+    def start_each(copy, order):
+        for t in order:
+            copy(t).start()
+
     @pl.when(stage == 0)
     def _():
         for c in range(x_pieces):
             own_copy(c).start()
-
-    up_copy(me).start()
-    for blocks in tables:
-        for _k, _size, copy in blocks:
-            copy.start()
-    for t in visits[1:]:
-        up_copy(t).start()
+        up_copy(me).start()
+
+    @pl.when(stage > 0)
+    def _():
+        start_tables(tables[0])
+        start_tables(tables[1])
+        start_each(up_copy, visits)
 
     barrier = pltpu.get_barrier_semaphore()
 
@@ -229,15 +237,12 @@
         def _():
             greet(lower)
 
-    fed = 2 + jnp.where(z < depth - 1, 1, 0) + jnp.where(z > 0, 1, 0)
-    pl.semaphore_wait(barrier, shards - 1 + jnp.where(stage < stages - 1, fed, 0))
-
     x_side = Spread(xs, x_send, x_recv, x_pieces, z, x, depth, stage == 0)
     a_side = Spread(act, a_send, a_recv, a_pieces, z, x, depth, stage >= 0)
 
     def hand_over(c, way, target):
         return pltpu.make_async_remote_copy(
-            src_ref=out_ref.at[c], dst_ref=xs.at[me, c],
+            src_ref=out_ref.at[:, pl.ds(pl.multiple_of(c * PIECE, LANES), PIECE)], dst_ref=xs.at[me, c],
             send_sem=h_send.at[way, c], recv_sem=x_recv.at[me, c],
             device_id={"pipe": (stage + 1) % stages, "tp": target}, device_id_type=MESH)
 
@@ -254,12 +259,6 @@
 
             do(hand_over(c, 2, partner))
             do(hand_over(c, 3, me))
-
-    @pl.when(stage == 0)
-    def _():
-        for c in range(x_pieces):
-            own_copy(c).wait()
-            x_side.forward(z, x, c)
 
     row_seg = lax.broadcasted_iota(jnp.int32, (rows, LANES), 0) // seg_rows
     lane_group = lax.broadcasted_iota(jnp.int32, (rows, LANES), 1) // rank
@@ -281,11 +280,10 @@
     fold_col = lax.broadcasted_iota(jnp.int32, (segments * LANES, LANES), 1)
     fold = jnp.where(fold_col == fold_row // LANES * rank + fold_row % rank, 1.0, 0.0).astype(bf16)
 
-    for blocks in tables:
-        for _k, _size, copy in blocks:
+    def panels(blocks, dest):
+        done = 0
+        for k, size, copy in blocks:
             copy.wait()
-    for blocks, dest in zip(tables, (shrink, expand)):
-        done = 0
         for k, size, copy in blocks:
             first = done
 
@@ -304,9 +302,6 @@
                 dest[pl.ds(at, PIECE), :] = panel.astype(bf16)
 
             done += size // flat
-
-    for t in visits:
-        down_copy(t).start()
 
     def raw(t, c):
         return xs[t, c].astype(f32)
@@ -338,65 +333,110 @@
                 part += lax.dot_general(left, up_tile(n, t, c), NT, preferred_element_type=f32)
             acc[:, block] = part if init else acc[:, block] + part
 
+    def own_up():
+        up_add([(me, c) for c in range(x_pieces)], True)
+
+    @pl.when(stage == 0)
+    def _():
+        for c in range(x_pieces):
+            own_copy(c).wait()
+        up_copy(me).wait()
+        start_tables(tables[0])
+        own_up()
+
+    fed = 2 + jnp.where(z < depth - 1, 1, 0) + jnp.where(z > 0, 1, 0)
+    pl.semaphore_wait(barrier, shards - 1 + jnp.where(stage < stages - 1, fed, 0))
+
+    @pl.when(stage == 0)
+    def _():
+        for c in range(x_pieces):
+            x_side.forward(z, x, c)
+        start_each(up_copy, visits[1:3])
+        panels(tables[0], shrink)
+
+    @pl.when(stage > 0)
+    def _():
+        panels(tables[0], shrink)
+        panels(tables[1], expand)
+        start_each(down_copy, visits)
+
     @pl.when(stage > 0)
     def _():
         for c in range(x_pieces):
             x_side.arrive(me, c)
-
-    up_copy(me).wait()
-    up_add([(me, c) for c in range(x_pieces)], True)
+        up_copy(me).wait()
+        own_up()
 
     def part_copy(owner, target):
         return pltpu.make_async_remote_copy(
             src_ref=partial.at[owner], dst_ref=partial.at[owner], send_sem=part_send.at[target],
             recv_sem=part_recv.at[owner], device_id={"tp": target}, device_id_type=MESH)
 
-    low = jnp.zeros((rows, LANES), f32)
-    for c in range(x_pieces):
-        low += jnp.dot(scaled(me, c, raw(me, c)), shrink[c * PIECE:(c + 1) * PIECE, :],
-                       preferred_element_type=f32)
-    low = jnp.where(in_segment, low, 0.0)
-    if rows < LANES:
-        low = jnp.concatenate([low, jnp.zeros((LANES - rows, LANES), f32)], axis=0)
-    turned = jnp.transpose(low)
-    picked = turned[0:rank]
-    for s in range(1, segments):
-        picked = picked + turned[s * rank:(s + 1) * rank]
-    partial[me] = picked
-
-    @pl.loop(1, shards)
-    def _(i):
-        part_copy(me, (me + i) % shards).start()
-
-    def spread_in(side, step, weights, pieces_of, add):
+    def send_part():
+        low = jnp.zeros((rows, LANES), f32)
+        for c in range(x_pieces):
+            low += jnp.dot(scaled(me, c, raw(me, c)), shrink[c * PIECE:(c + 1) * PIECE, :],
+                           preferred_element_type=f32)
+        low = jnp.where(in_segment, low, 0.0)
+        if rows < LANES:
+            low = jnp.concatenate([low, jnp.zeros((LANES - rows, LANES), f32)], axis=0)
+        turned = jnp.transpose(low)
+        picked = turned[0:rank]
+        for s in range(1, segments):
+            picked = picked + turned[s * rank:(s + 1) * rank]
+        partial[me] = picked
+
+        @pl.loop(1, shards)
+        def _(i):
+            part_copy(me, (me + i) % shards).start()
+
+    def spread_in(side, step, weights, pieces_of, add, group):
         for t in weights:
             t.wait()
 
-        @pl.loop(0, side.pieces)
-        def _(c):
-            side.relay(step, x, c)
-
-            @pl.when(c < side.pieces - 1)
-            def _():
-                side.arrive(shard(step - 1, True), c)
-
-            @pl.when(c == side.pieces - 1)
-            def _():
-                side.relay(step - 1, 1 - x, c)
-
-            add([(t, c) for t in pieces_of])
+        @pl.loop(0, side.pieces // group)
+        def _(j):
+            for g in range(group):
+                c = j * group + g
+                side.relay(step, x, c)
+
+                @pl.when(c < side.pieces - 1)
+                def _():
+                    side.arrive(shard(step - 1, True), c)
+
+                @pl.when(c == side.pieces - 1)
+                def _():
+                    side.relay(step - 1, 1 - x, c)
+
+            add([(t, j * group + g) for t in pieces_of for g in range(group)])
+
+    send_part()
 
     for i in range(1, depth):
         fresh = [shard(i - 1, True), shard(i, False)]
-        spread_in(x_side, i, [up_copy(t) for t in fresh], fresh, lambda items: up_add(items, False))
+
+        @pl.when(stage == 0)
+        def _():
+            if i == 1:
+                start_tables(tables[1])
+            if i == 2:
+                start_each(up_copy, visits[6:])
+            if i == depth - 1:
+                start_each(down_copy, visits[:3])
+
+        spread_in(x_side, i, [up_copy(t) for t in fresh], fresh, lambda items: up_add(items, False),
+                  2 if x_pieces % 2 == 0 else 1)
+        if i == 1:
+            @pl.when(stage == 0)
+            def _():
+                start_each(up_copy, visits[3:6])
+                panels(tables[1], expand)
 
     last = shard(depth - 1, True)
     up_copy(last).wait()
-
-    @pl.loop(0, x_pieces - 2)
-    def _(c):
+    for c in range(x_pieces - 2):
         x_side.arrive(last, c)
-        up_add([(last, c)], False)
+    up_add([(last, c) for c in range(x_pieces - 2)], False)
 
     @pl.loop(1, shards)
     def _(i):
@@ -408,6 +448,10 @@
         summed = summed + partial[t]
     stacked = jnp.concatenate([summed] * segments + [jnp.zeros((LANES - segments * rank, LANES), f32)], axis=0)
     low = jnp.where(in_segment, jnp.transpose(stacked)[:rows], 0.0)
+
+    @pl.when(stage == 0)
+    def _():
+        start_each(down_copy, visits[3:5])
 
     x_side.arrive(last, x_pieces - 2)
     x_side.relay(depth - 1, 1 - x, x_pieces - 1)
@@ -443,6 +487,10 @@
                 part += lax.dot_general(act[t, c], down_tile(n, t, c), NT, preferred_element_type=f32)
             acc[:, block] = acc[:, block] + part
 
+    @pl.when(stage == 0)
+    def _():
+        start_each(down_copy, visits[5:])
+
     for n in range(x_pieces):
         acc[:, n * PIECE:(n + 1) * PIECE] = xs[me, n].astype(f32)
 
@@ -450,7 +498,7 @@
     for i in range(1, depth):
         fresh = [shard(i - 1, True), shard(i, False)]
         spread_in(a_side, i, [down_copy(t) for t in fresh],
-                  ([me] if i == 1 else []) + fresh, down_add)
+                  ([me] if i == 1 else []) + fresh, down_add, 1)
 
     down_copy(last).wait()
 
@@ -472,7 +520,7 @@
         part = jnp.zeros((rows, PIECE), f32)
         for c in (a_pieces - 2, a_pieces - 1):
             part += lax.dot_general(act[last, c], down_tile(n, last, c), NT, preferred_element_type=f32)
-        out_ref[n] = jnp.where(kept, acc[:, block] + part, 0.0).astype(bf16)
+        out_ref[:, block] = jnp.where(kept, acc[:, block] + part, 0.0).astype(bf16)
         hand_each(n, lambda d: d.start())
 
     @pl.loop(0, x_pieces)
@@ -499,9 +547,9 @@
     dma = pltpu.SemaphoreType.DMA
     flat = PIECE * rank
     blocks = table_blocks(shards * hidden // flat * flat, shrink_weight, expand_weight)
-    pieces = pl.pallas_call(
+    return pl.pallas_call(
         section_kernel,
-        out_shape=jax.ShapeDtypeStruct((x_pieces, rows, PIECE), jnp.bfloat16),
+        out_shape=jax.ShapeDtypeStruct((rows, cols), jnp.bfloat16),
         in_specs=[smem, smem, vmem] + [hbm] * 5,
         out_specs=vmem,
         scratch_shapes=[
@@ -524,7 +572,6 @@
             collective_id=0, has_side_effects=True, vmem_limit_bytes=VMEM_BYTES
         ),
     )(ids, live, gain[None, :], current, shrink_weight, expand_weight, up_weight, down_weight)
-    return pieces.transpose(1, 0, 2).reshape(rows, cols)
 
 
 def table_blocks(width, *tables):

time: 99.5 us -> 90 us (0.905)
  Pallas kernels: 97.3 us -> 88.2 us
    pallas_call x1, Pallas kernels: 97.3 us -> 88.2 us  [fused_sections(): pl.pallas_call(section_kernel, out_shape=jax.ShapeDtypeStruct((rows, cols...]
    unnamed x0 -> x1, local copies, waits for them, and re-layouts: none -> 1.65 us
    transpose x1 -> x0, local copies, waits for them, and re-layouts: 1.04 us -> none  [fused_sections(): return pieces.transpose(1, 0, 2).reshape(rows, cols)]
where the time goes in v2:
time: 90 us; the launch traced here: 89.8 us
  Pallas kernels  88.2 us (98%)
  local copies, waits for them, and re-layouts  1.65 us (2%)
    pallas_call x1, Pallas kernels, fused_sections(): pl.pallas_call(section_kernel, out_shape=jax.ShapeDtypeStruct((rows, cols...  88.2 us

profile of v2, /device:TPU:1, one launch (start us, length us, event | category | flops | bytes accessed | tf_op | source)
XLA Modules:
  0.0 89.8 jit_solution(4955431495331597687)
XLA Ops:
  0.0 88.2 %shard_map.82 = bf16[120,1024]{1,0:T(8,128)(2,1)} custom-call(s32[3]{0:T(128)} %bitcast.14, s32[3]{0:T(128)} %bitcast.15, f32[1,8192]{1,0:T(1,128)} %gain_ref.1, bf16[120,1024]{1,0:T(8,128)(2,1)} %bitcast.13, bf16[128,16384]{1,0:T(8,128)(2,1)} %bitcast.11, bf16[128,28672]{1,0:T(8,128)(2,1)} %bitcast.10, bf16[1792,8192]{1,0:T(8,128)(2,1)} %bitcast.8, ...), custom_call_target="tpu_custom_call" | custom-call | tf_op jit(solution)/shard_map/pallas_call | solution.py:550
  88.2 1.7 %copy.10 = bf16[1,1,120,1024]{3,2,1,0:T(8,128)(2,1)} copy(bf16[1,1,120,1024]{3,2,1,0:T(8,128)(2,1)} %bitcast.12) | data formatting | bytes 491520

commit v3 on v2

--- a/solution.py
+++ b/solution.py
@@ -76,66 +76,95 @@
 
 
 class Spread:
+    OWN, ALONG, EXTRA, ACROSS = range(4)
+
     def __init__(self, buf, send, recv, pieces, z, x, depth, starts_own):
         self.buf, self.send, self.recv, self.pieces = buf, send, recv, pieces
         self.z, self.x, self.depth, self.starts_own = z, x, depth, starts_own
         self.shards = depth * COLUMNS
         self.me = z * COLUMNS + x
 
-    def copy(self, t, c, way, target):
+    def copy(self, t, c, kind, target):
         return pltpu.make_async_remote_copy(
             src_ref=self.buf.at[t, c], dst_ref=self.buf.at[t, c],
-            send_sem=self.send.at[way, t, c], recv_sem=self.recv.at[t, c],
+            send_sem=self.send.at[kind], recv_sem=self.recv.at[t, c],
             device_id={"tp": target}, device_id_type=MESH)
 
-    def each(self, source_z, column, c, do):
-        z, x, me = self.z, self.x, self.me
-        t = source_z * COLUMNS + column
-        own, special = column == x, c == self.pieces - 1
-        along = jnp.logical_or(own, special)
-        across = jnp.logical_and(own, jnp.logical_or(c != self.pieces - 1, source_z == z))
-
-        @pl.when(jnp.logical_and(along, jnp.logical_and(source_z <= z, z < self.depth - 1)))
+    def start_along(self, source_z, t, c, kind):
+        z, me = self.z, self.me
+
+        @pl.when(jnp.logical_and(source_z <= z, z < self.depth - 1))
         def _():
-            do(self.copy(t, c, 0, (me + COLUMNS) % self.shards))
-
-        @pl.when(jnp.logical_and(along, jnp.logical_and(source_z >= z, z > 0)))
+            self.copy(t, c, kind, (me + COLUMNS) % self.shards).start()
+
+        @pl.when(jnp.logical_and(source_z >= z, z > 0))
         def _():
-            do(self.copy(t, c, 1, (me + self.shards - COLUMNS) % self.shards))
-
-        @pl.when(across)
-        def _():
-            do(self.copy(t, c, 2, z * COLUMNS + (1 - x)))
-
-    def forward(self, source_z, column, c):
-        self.each(source_z, column, c, lambda d: d.start())
+            self.copy(t, c, kind, (me + self.shards - COLUMNS) % self.shards).start()
+
+    def start_across(self, t, c, kind):
+        self.copy(t, c, kind, self.z * COLUMNS + (1 - self.x)).start()
+
+    def start_own(self, c):
+        self.start_along(self.z, self.me, c, self.OWN)
+        self.start_across(self.me, c, self.OWN)
 
     def arrive(self, t, c):
-        self.copy(t, c, 2, self.z * COLUMNS + (1 - self.x)).wait_recv()
-
-    def relay(self, step, column, c):
+        self.copy(t, c, self.ACROSS, self.z * COLUMNS + (1 - self.x)).wait_recv()
+
+    def both_sides(self, step, do):
         for source_z in (self.z - step, self.z + step) if step else (self.z,):
             @pl.when(jnp.logical_and(source_z >= 0, source_z < self.depth))
             def _():
-                self.arrive(source_z * COLUMNS + column, c)
-                self.forward(source_z, column, c)
-
-    def drain(self):
-        @pl.loop(0, self.depth)
-        def _(source_z):
-            @pl.when(jnp.logical_or(source_z != self.z, self.starts_own))
+                do(source_z)
+
+    def relay(self, step, c):
+        def do(source_z):
+            t = source_z * COLUMNS + self.x
+            self.arrive(t, c)
+            self.start_along(source_z, t, c, self.ALONG)
+
+            @pl.when(c < self.pieces - 1)
             def _():
-                @pl.loop(0, self.pieces)
-                def _(c):
-                    self.each(source_z, self.x, c, lambda d: d.wait_send())
-
-            self.each(source_z, 1 - self.x, self.pieces - 1, lambda d: d.wait_send())
+                self.start_across(t, c, self.ACROSS)
+
+        self.both_sides(step, do)
+
+    def relay_extra(self, step):
+        def do(source_z):
+            t = source_z * COLUMNS + 1 - self.x
+            self.arrive(t, self.pieces - 1)
+            self.start_along(source_z, t, self.pieces - 1, self.EXTRA)
+
+        self.both_sides(step, do)
+
+    def sent(self, kind, outer, inner, filler):
+        if outer and inner:
+            view = filler.at[0:outer, 0:inner]
+            pltpu.make_async_remote_copy(
+                src_ref=view, dst_ref=view, send_sem=self.send.at[kind], recv_sem=self.recv.at[0, 0],
+                device_id={"tp": self.me}, device_id_type=MESH).wait_send()
+
+    def drain(self, filler):
+        for z in range(self.depth):
+            ways = (z < self.depth - 1) + (z > 0)
+            layers = (z + 1) * (z < self.depth - 1) + (self.depth - z) * (z > 0)
+
+            @pl.when(self.z == z)
+            def _():
+                @pl.when(self.starts_own)
+                def _():
+                    self.sent(self.OWN, ways + 1, self.pieces, filler)
+
+                self.sent(self.ALONG, layers - ways, self.pieces, filler)
+                self.sent(self.EXTRA, layers, 1, filler)
+
+        self.sent(self.ACROSS, self.depth - 1, self.pieces - 1, filler)
 
 
 def section_kernel(
-    ids_ref, live_ref, gain_ref, x_hbm, reduce_hbm, expand_hbm, up_hbm, down_hbm, out_ref,
-    up_v, down_v, xs, act, acc, sq, shrink, expand, partial,
-    up_sem, down_sem, tab_sem, own_sem, part_send, part_recv, x_send, x_recv, a_send, a_recv, h_send,
+    ids_ref, live_ref, gain_ref, x_hbm, reduce_hbm, expand_hbm, up_hbm, down_hbm, out_hbm,
+    up_v, down_v, xs, act, acc, sq, shrink, expand, partial, out_v,
+    up_sem, down_sem, tab_sem, own_sem, part_send, part_recv, x_send, x_recv, a_send, a_recv, h_send, out_sem,
 ):
     shards, x_pieces, rows, _ = xs.shape
     a_pieces = act.shape[1]
@@ -180,7 +209,7 @@
         return pltpu.make_async_copy(down_hbm.at[:, span], down_v.at[:, span], down_sem.at[t])
 
     def own_copy(c):
-        return pltpu.make_async_copy(x_hbm.at[:, c * PIECE:(c + 1) * PIECE], xs.at[me, c], own_sem.at[c])
+        return pltpu.make_async_copy(x_hbm.at[:, c * PIECE:(c + 1) * PIECE], xs.at[me, c], own_sem.at[0])
 
     tables = []
     for table, length in ((reduce_hbm, shrink_len), (expand_hbm, expand_len)):
@@ -240,25 +269,38 @@
     x_side = Spread(xs, x_send, x_recv, x_pieces, z, x, depth, stage == 0)
     a_side = Spread(act, a_send, a_recv, a_pieces, z, x, depth, stage >= 0)
 
-    def hand_over(c, way, target):
+    def hand_over(c, target):
         return pltpu.make_async_remote_copy(
-            src_ref=out_ref.at[:, pl.ds(pl.multiple_of(c * PIECE, LANES), PIECE)], dst_ref=xs.at[me, c],
-            send_sem=h_send.at[way, c], recv_sem=x_recv.at[me, c],
+            src_ref=out_v.at[c], dst_ref=xs.at[me, c], send_sem=h_send.at[0], recv_sem=x_recv.at[me, c],
             device_id={"pipe": (stage + 1) % stages, "tp": target}, device_id_type=MESH)
 
-    def hand_each(c, do):
+    def hand_each(c):
         @pl.when(stage < stages - 1)
         def _():
             @pl.when(z < depth - 1)
             def _():
-                do(hand_over(c, 0, upper))
+                hand_over(c, upper).start()
 
             @pl.when(z > 0)
             def _():
-                do(hand_over(c, 1, lower))
-
-            do(hand_over(c, 2, partner))
-            do(hand_over(c, 3, me))
+                hand_over(c, lower).start()
+
+            hand_over(c, partner).start()
+            hand_over(c, me).start()
+
+    def hand_drain():
+        for at in range(depth):
+            count = 2 + (at < depth - 1) + (at > 0)
+
+            @pl.when(jnp.logical_and(stage < stages - 1, z == at))
+            def _():
+                view = xs.at[0:count]
+                pltpu.make_async_remote_copy(
+                    src_ref=view, dst_ref=view, send_sem=h_send.at[0], recv_sem=x_recv.at[0, 0],
+                    device_id={"tp": me}, device_id_type=MESH).wait_send()
+
+    def out_copy(c):
+        return pltpu.make_async_copy(out_v.at[c], out_hbm.at[:, c * PIECE:(c + 1) * PIECE], out_sem.at[0])
 
     row_seg = lax.broadcasted_iota(jnp.int32, (rows, LANES), 0) // seg_rows
     lane_group = lax.broadcasted_iota(jnp.int32, (rows, LANES), 1) // rank
@@ -318,7 +360,11 @@
         at = pl.multiple_of(t * cols + c * PIECE, LANES)
         return up_v[n * PIECE:(n + 1) * PIECE, pl.ds(at, PIECE)]
 
-    def up_add(items, init):
+    def up_dot(left, n, t, c, flipped):
+        dims = (((1,), (0,)), ((), ())) if flipped else NT
+        return lax.dot_general(left, up_tile(n, t, c), dims, preferred_element_type=f32)
+
+    def up_add(items, init, flipped):
         lefts = []
         total = jnp.zeros((rows, LANES), f32) if init else sq[...]
         for t, c in items:
@@ -330,47 +376,35 @@
             block = slice(n * PIECE, (n + 1) * PIECE)
             part = jnp.zeros((rows, PIECE), f32)
             for (t, c), left in zip(items, lefts):
-                part += lax.dot_general(left, up_tile(n, t, c), NT, preferred_element_type=f32)
+                part += up_dot(left, n, t, c, flipped)
             acc[:, block] = part if init else acc[:, block] + part
 
-    def own_up():
-        up_add([(me, c) for c in range(x_pieces)], True)
-
-    @pl.when(stage == 0)
-    def _():
-        for c in range(x_pieces):
-            own_copy(c).wait()
-        up_copy(me).wait()
-        start_tables(tables[0])
-        own_up()
-
-    fed = 2 + jnp.where(z < depth - 1, 1, 0) + jnp.where(z > 0, 1, 0)
-    pl.semaphore_wait(barrier, shards - 1 + jnp.where(stage < stages - 1, fed, 0))
-
-    @pl.when(stage == 0)
-    def _():
-        for c in range(x_pieces):
-            x_side.forward(z, x, c)
-        start_each(up_copy, visits[1:3])
-        panels(tables[0], shrink)
-
-    @pl.when(stage > 0)
-    def _():
-        panels(tables[0], shrink)
-        panels(tables[1], expand)
-        start_each(down_copy, visits)
-
-    @pl.when(stage > 0)
-    def _():
-        for c in range(x_pieces):
-            x_side.arrive(me, c)
-        up_copy(me).wait()
-        own_up()
+    def per_stage(work):
+        @pl.when(stage == 0)
+        def _():
+            work(False)
+
+        @pl.when(stage > 0)
+        def _():
+            work(True)
+
+    def own_up(flipped):
+        up_add([(me, c) for c in range(x_pieces)], True, flipped)
+
+    def flip_up():
+        for t in visits:
+            up_copy(t).wait()
+
+        @pl.loop(0, a_pieces * shards * x_pieces)
+        def _(i):
+            tall = pl.ds(pl.multiple_of(i // (shards * x_pieces) * PIECE, PIECE), PIECE)
+            wide = pl.ds(pl.multiple_of(i % (shards * x_pieces) * PIECE, PIECE), PIECE)
+            up_v[tall, wide] = jnp.transpose(up_v[tall, wide])
 
     def part_copy(owner, target):
         return pltpu.make_async_remote_copy(
-            src_ref=partial.at[owner], dst_ref=partial.at[owner], send_sem=part_send.at[target],
-            recv_sem=part_recv.at[owner], device_id={"tp": target}, device_id_type=MESH)
+            src_ref=partial.at[owner], dst_ref=partial.at[owner], send_sem=part_send.at[0],
+            recv_sem=part_recv.at[0], device_id={"tp": target}, device_id_type=MESH)
 
     def send_part():
         low = jnp.zeros((rows, LANES), f32)
@@ -390,15 +424,43 @@
         def _(i):
             part_copy(me, (me + i) % shards).start()
 
-    def spread_in(side, step, weights, pieces_of, add, group):
-        for t in weights:
-            t.wait()
-
+    @pl.when(stage == 0)
+    def _():
+        pltpu.make_async_copy(xs.at[me], xs.at[me], own_sem.at[0]).wait()
+        up_copy(me).wait()
+        start_tables(tables[0])
+        own_up(False)
+        start_each(up_copy, visits[1:3])
+
+    fed = 2 + jnp.where(z < depth - 1, 1, 0) + jnp.where(z > 0, 1, 0)
+    pl.semaphore_wait(barrier, shards - 1 + jnp.where(stage < stages - 1, fed, 0))
+
+    @pl.when(stage == 0)
+    def _():
+        for c in range(x_pieces):
+            x_side.start_own(c)
+        panels(tables[0], shrink)
+        send_part()
+
+    @pl.when(stage > 0)
+    def _():
+        panels(tables[0], shrink)
+        panels(tables[1], expand)
+        start_each(down_copy, visits)
+        flip_up()
+
+    @pl.when(stage > 0)
+    def _():
+        for c in range(x_pieces):
+            x_side.arrive(me, c)
+        own_up(True)
+
+    def spread_in(side, step, pieces_of, add, group):
         @pl.loop(0, side.pieces // group)
         def _(j):
             for g in range(group):
                 c = j * group + g
-                side.relay(step, x, c)
+                side.relay(step, c)
 
                 @pl.when(c < side.pieces - 1)
                 def _():
@@ -406,17 +468,17 @@
 
                 @pl.when(c == side.pieces - 1)
                 def _():
-                    side.relay(step - 1, 1 - x, c)
+                    side.relay_extra(step - 1)
 
             add([(t, j * group + g) for t in pieces_of for g in range(group)])
-
-    send_part()
 
     for i in range(1, depth):
         fresh = [shard(i - 1, True), shard(i, False)]
 
         @pl.when(stage == 0)
         def _():
+            for t in fresh:
+                up_copy(t).wait()
             if i == 1:
                 start_tables(tables[1])
             if i == 2:
@@ -424,24 +486,32 @@
             if i == depth - 1:
                 start_each(down_copy, visits[:3])
 
-        spread_in(x_side, i, [up_copy(t) for t in fresh], fresh, lambda items: up_add(items, False),
-                  2 if x_pieces % 2 == 0 else 1)
+        spread_in(x_side, i, fresh, lambda items: per_stage(functools.partial(up_add, items, False)), 2 if x_pieces % 2 == 0 else 1)
         if i == 1:
             @pl.when(stage == 0)
             def _():
                 start_each(up_copy, visits[3:6])
                 panels(tables[1], expand)
 
+            @pl.when(stage > 0)
+            def _():
+                send_part()
+
     last = shard(depth - 1, True)
-    up_copy(last).wait()
+
+    @pl.when(stage == 0)
+    def _():
+        up_copy(last).wait()
+
     for c in range(x_pieces - 2):
         x_side.arrive(last, c)
-    up_add([(last, c) for c in range(x_pieces - 2)], False)
-
-    @pl.loop(1, shards)
-    def _(i):
-        owner = (me + i) % shards
-        part_copy(owner, owner).wait_recv()
+    per_stage(functools.partial(up_add, [(last, c) for c in range(x_pieces - 2)], False))
+
+    others = partial.at[0:shards - 1]
+    all_parts = pltpu.make_async_remote_copy(
+        src_ref=others, dst_ref=others, send_sem=part_send.at[0], recv_sem=part_recv.at[0],
+        device_id={"tp": me}, device_id_type=MESH)
+    all_parts.wait_recv()
 
     summed = partial[0]
     for t in range(1, shards):
@@ -454,7 +524,7 @@
         start_each(down_copy, visits[3:5])
 
     x_side.arrive(last, x_pieces - 2)
-    x_side.relay(depth - 1, 1 - x, x_pieces - 1)
+    x_side.relay_extra(depth - 1)
     finals = [(last, x_pieces - 2), (last, x_pieces - 1)]
     square = sq[...]
     lefts = []
@@ -465,15 +535,18 @@
     inverse = lax.rsqrt(jnp.sum(square, axis=1, keepdims=True) / width + EPSILON)
     low_rank = (low * inverse).astype(bf16)
 
-    for n in range(a_pieces):
-        block = slice(n * PIECE, (n + 1) * PIECE)
-        base = jnp.zeros((rows, PIECE), f32)
-        for (t, c), left in zip(finals, lefts):
-            base += lax.dot_general(left, up_tile(n, t, c), NT, preferred_element_type=f32)
-        adapted = lax.dot_general(low_rank, expand[block, :], NT, preferred_element_type=f32)
-        value = inverse * (acc[:, block] + base) + adapted
-        act[me, n] = (value / (1.0 + jnp.exp(-value))).astype(bf16)
-        a_side.forward(z, x, n)
+    def up_finish(flipped):
+        for n in range(a_pieces):
+            block = slice(n * PIECE, (n + 1) * PIECE)
+            base = jnp.zeros((rows, PIECE), f32)
+            for (t, c), left in zip(finals, lefts):
+                base += up_dot(left, n, t, c, flipped)
+            adapted = lax.dot_general(low_rank, expand[block, :], NT, preferred_element_type=f32)
+            value = inverse * (acc[:, block] + base) + adapted
+            act[me, n] = (value / (1.0 + jnp.exp(-value))).astype(bf16)
+            a_side.start_own(n)
+
+    per_stage(up_finish)
 
     def down_tile(n, t, c):
         at = pl.multiple_of(t * hidden + c * PIECE, LANES)
@@ -497,8 +570,9 @@
     down_copy(me).wait()
     for i in range(1, depth):
         fresh = [shard(i - 1, True), shard(i, False)]
-        spread_in(a_side, i, [down_copy(t) for t in fresh],
-                  ([me] if i == 1 else []) + fresh, down_add, 1)
+        for t in fresh:
+            down_copy(t).wait()
+        spread_in(a_side, i, ([me] if i == 1 else []) + fresh, down_add, 1)
 
     down_copy(last).wait()
 
@@ -514,25 +588,21 @@
         kept = jnp.logical_or(kept, jnp.logical_and(row >= start, row < start + jnp.minimum(live_ref[s], seg_rows)))
 
     a_side.arrive(last, a_pieces - 2)
-    a_side.relay(depth - 1, 1 - x, a_pieces - 1)
+    a_side.relay_extra(depth - 1)
     for n in range(x_pieces):
         block = slice(n * PIECE, (n + 1) * PIECE)
         part = jnp.zeros((rows, PIECE), f32)
         for c in (a_pieces - 2, a_pieces - 1):
             part += lax.dot_general(act[last, c], down_tile(n, last, c), NT, preferred_element_type=f32)
-        out_ref[:, block] = jnp.where(kept, acc[:, block] + part, 0.0).astype(bf16)
-        hand_each(n, lambda d: d.start())
-
-    @pl.loop(0, x_pieces)
-    def _(c):
-        hand_each(c, lambda d: d.wait_send())
-
-    @pl.loop(1, shards)
-    def _(i):
-        part_copy(me, (me + i) % shards).wait_send()
-
-    x_side.drain()
-    a_side.drain()
+        out_v[n] = jnp.where(kept, acc[:, block] + part, 0.0).astype(bf16)
+        hand_each(n)
+        out_copy(n).start()
+
+    all_parts.wait_send()
+    x_side.drain(act)
+    a_side.drain(act)
+    hand_drain()
+    pltpu.make_async_copy(out_v, out_v, out_sem.at[0]).wait()
 
 
 def fused_sections(current, ids, live, gain, up_weight, down_weight, shrink_weight, expand_weight):
@@ -551,7 +621,7 @@
         section_kernel,
         out_shape=jax.ShapeDtypeStruct((rows, cols), jnp.bfloat16),
         in_specs=[smem, smem, vmem] + [hbm] * 5,
-        out_specs=vmem,
+        out_specs=hbm,
         scratch_shapes=[
             pltpu.VMEM(up_weight.shape, jnp.bfloat16),
             pltpu.VMEM(down_weight.shape, jnp.bfloat16),
@@ -562,11 +632,12 @@
             pltpu.VMEM((cols, LANES), jnp.bfloat16),
             pltpu.VMEM((hidden, LANES), jnp.bfloat16),
             pltpu.VMEM((shards, rank, LANES), jnp.float32),
-            dma((shards,)), dma((shards,)), dma((blocks,)), dma((x_pieces,)),
-            dma((shards,)), dma((shards,)),
-            dma((3, shards, x_pieces)), dma((shards, x_pieces)),
-            dma((3, shards, a_pieces)), dma((shards, a_pieces)),
-            dma((4, x_pieces)),
+            pltpu.VMEM((x_pieces, rows, PIECE), jnp.bfloat16),
+            dma((shards,)), dma((shards,)), dma((blocks,)), dma((1,)),
+            dma((1,)), dma((1,)),
+            dma((4,)), dma((shards, x_pieces)),
+            dma((4,)), dma((shards, a_pieces)),
+            dma((1,)), dma((1,)),
         ],
         compiler_params=pltpu.CompilerParams(
             collective_id=0, has_side_effects=True, vmem_limit_bytes=VMEM_BYTES

time: 90 us -> 84.4 us (0.938)
  Pallas kernels: 88.2 us -> 82.6 us
    pallas_call x1, Pallas kernels: 88.2 us -> 82.6 us  [fused_sections(): pl.pallas_call(section_kernel, out_shape=jax.ShapeDtypeStruct((rows, cols...]
where the time goes in v3:
time: 84.4 us; the launch traced here: 84.2 us
  Pallas kernels  82.6 us (98%)
  local copies, waits for them, and re-layouts  1.65 us (2%)
    pallas_call x1, Pallas kernels, fused_sections(): pl.pallas_call(section_kernel, out_shape=jax.ShapeDtypeStruct((rows, cols...  82.6 us

profile of v3, /device:TPU:1, one launch (start us, length us, event | category | flops | bytes accessed | tf_op | source)
XLA Modules:
  0.0 84.2 jit_solution(8656862967315093203)
XLA Ops:
  0.0 82.6 %shard_map.82 = bf16[120,1024]{1,0:T(8,128)(2,1)} custom-call(s32[3]{0:T(128)} %bitcast.14, s32[3]{0:T(128)} %bitcast.15, f32[1,8192]{1,0:T(1,128)} %gain_ref.1, bf16[120,1024]{1,0:T(8,128)(2,1)} %bitcast.13, bf16[128,16384]{1,0:T(8,128)(2,1)} %bitcast.11, bf16[128,28672]{1,0:T(8,128)(2,1)} %bitcast.10, bf16[1792,8192]{1,0:T(8,128)(2,1)} %bitcast.8, ...), custom_call_target="tpu_custom_call" | custom-call | tf_op jit(solution)/shard_map/pallas_call | solution.py:620
  82.6 1.7 %copy.10 = bf16[1,1,120,1024]{3,2,1,0:T(8,128)(2,1)} copy(bf16[1,1,120,1024]{3,2,1,0:T(8,128)(2,1)} %bitcast.12) | data formatting | bytes 491520

commit v4 on v3

--- a/solution.py
+++ b/solution.py
@@ -211,17 +211,44 @@
     def own_copy(c):
         return pltpu.make_async_copy(x_hbm.at[:, c * PIECE:(c + 1) * PIECE], xs.at[me, c], own_sem.at[0])
 
-    tables = []
-    for table, length in ((reduce_hbm, shrink_len), (expand_hbm, expand_len)):
-        blocks = []
-        for at in range(0, length, table_width):
-            size = min(table_width, length - at)
-            k = sum(len(t) for t in tables) + len(blocks)
-            copy = pltpu.make_async_copy(
-                table.at[:, at:at + size],
-                down_v.at[k * adapters:(k + 1) * adapters, 0:size], tab_sem.at[k])
-            blocks.append((k, size, copy))
-        tables.append(blocks)
+    inner = jnp.logical_and(z > 0, z < depth - 1)
+    near_other, second_other, last = shard(1, True), shard(2, True), shard(3, True)
+    second_turn = jnp.where(inner, shard(3, False), near_other)
+    third_turn = jnp.where(inner, near_other, shard(3, False))
+    down_early = [me, partner, shard(1, False), second_turn, shard(2, False)]
+    down_late = [third_turn, second_other, last]
+    flat = PIECE * rank
+    lane_tiles = flat // LANES
+
+    shrink_blocks = []
+    for k, at in enumerate(range(0, shrink_len, table_width)):
+        size = min(table_width, shrink_len - at)
+        copy = pltpu.make_async_copy(
+            reduce_hbm.at[:, at:at + size],
+            down_v.at[k * adapters:(k + 1) * adapters, 0:size], tab_sem.at[k])
+        shrink_blocks.append((k, size, copy))
+    bands = range(len(shrink_blocks), cols // adapters)
+    spots = [(t, band) for t in down_late for band in bands]
+    whole, rest = flat // hidden, flat % hidden
+    per_spot = hidden // rest if rest else 1
+
+    def expand_parts(n):
+        parts = [(j * hidden, hidden, spots[n * whole + j], 0) for j in range(whole)]
+        if rest:
+            spot_of = spots[a_pieces * whole + n // per_spot]
+            parts.append((whole * hidden, rest, spot_of, n % per_spot * rest))
+        views = []
+        for at, size, (t, band), shift in parts:
+            lanes = pl.ds(pl.multiple_of(t * hidden + shift, LANES), size)
+            views.append((n * flat + at, size, (slice(band * adapters, (band + 1) * adapters), lanes)))
+        return views
+
+    def start_expand():
+        for n in range(a_pieces):
+            for at, size, (band, lanes) in expand_parts(n):
+                pltpu.make_async_copy(
+                    expand_hbm.at[:, at:at + size], down_v.at[band, lanes],
+                    tab_sem.at[len(shrink_blocks) + n]).start()
 
     def start_tables(blocks):
         for _k, _size, copy in blocks:
@@ -239,8 +266,8 @@
 
     @pl.when(stage > 0)
     def _():
-        start_tables(tables[0])
-        start_tables(tables[1])
+        start_tables(shrink_blocks)
+        start_expand()
         start_each(up_copy, visits)
 
     barrier = pltpu.get_barrier_semaphore()
@@ -313,8 +340,6 @@
         hit = jnp.logical_and(pick_row // 8 == s, pick_col == ids_ref[s])
         picks = jnp.where(hit, 1.0, picks)
     picks = picks.astype(bf16)
-    flat = PIECE * rank
-    lane_tiles = flat // LANES
     spot_row = lax.broadcasted_iota(jnp.int32, (PIECE, LANES), 0) % 8
     spot_lane = lax.broadcasted_iota(jnp.int32, (PIECE, LANES), 1) // rank
     spot = spot_row == spot_lane
@@ -322,28 +347,36 @@
     fold_col = lax.broadcasted_iota(jnp.int32, (segments * LANES, LANES), 1)
     fold = jnp.where(fold_col == fold_row // LANES * rank + fold_row % rank, 1.0, 0.0).astype(bf16)
 
-    def panels(blocks, dest):
+    def panel_of(table):
+        got = jnp.dot(picks, table, preferred_element_type=f32)
+        parts = []
+        for s in range(segments):
+            tall = jnp.concatenate(
+                [got[8 * s:8 * s + 8, LANES * i:LANES * (i + 1)] for i in range(lane_tiles)], axis=0)
+            parts.append(jnp.where(spot, tall, 0.0).astype(bf16))
+        return jnp.dot(jnp.concatenate(parts, axis=1), fold, preferred_element_type=f32).astype(bf16)
+
+    def shrink_panels(then):
+        for k, size, copy in shrink_blocks:
+            copy.wait()
+        start_each(up_copy, then)
         done = 0
-        for k, size, copy in blocks:
-            copy.wait()
-        for k, size, copy in blocks:
+        for k, size, copy in shrink_blocks:
             first = done
 
             @pl.loop(0, size // flat)
             def _(j):
                 span = pl.ds(pl.multiple_of(j * flat, LANES), flat)
-                table = down_v[k * adapters:(k + 1) * adapters, span]
-                got = jnp.dot(picks, table, preferred_element_type=f32)
-                parts = []
-                for s in range(segments):
-                    tall = jnp.concatenate(
-                        [got[8 * s:8 * s + 8, LANES * i:LANES * (i + 1)] for i in range(lane_tiles)], axis=0)
-                    parts.append(jnp.where(spot, tall, 0.0).astype(bf16))
-                panel = jnp.dot(jnp.concatenate(parts, axis=1), fold, preferred_element_type=f32)
                 at = pl.multiple_of((first + j) * PIECE, PIECE)
-                dest[pl.ds(at, PIECE), :] = panel.astype(bf16)
+                shrink[pl.ds(at, PIECE), :] = panel_of(down_v[k * adapters:(k + 1) * adapters, span])
 
             done += size // flat
+
+    def expand_panel(n):
+        landed = down_v.at[0:adapters, 0:flat]
+        pltpu.make_async_copy(landed, landed, tab_sem.at[len(shrink_blocks) + n]).wait()
+        table = jnp.concatenate([down_v[band, lanes] for _at, _size, (band, lanes) in expand_parts(n)], axis=1)
+        expand[n * PIECE:(n + 1) * PIECE, :] = panel_of(table)
 
     def raw(t, c):
         return xs[t, c].astype(f32)
@@ -428,7 +461,7 @@
     def _():
         pltpu.make_async_copy(xs.at[me], xs.at[me], own_sem.at[0]).wait()
         up_copy(me).wait()
-        start_tables(tables[0])
+        start_tables(shrink_blocks)
         own_up(False)
         start_each(up_copy, visits[1:3])
 
@@ -439,14 +472,15 @@
     def _():
         for c in range(x_pieces):
             x_side.start_own(c)
-        panels(tables[0], shrink)
+        shrink_panels(visits[3:5])
         send_part()
 
     @pl.when(stage > 0)
     def _():
-        panels(tables[0], shrink)
-        panels(tables[1], expand)
-        start_each(down_copy, visits)
+        shrink_panels([])
+        for n in range(a_pieces):
+            expand_panel(n)
+        start_each(down_copy, down_early + down_late)
         flip_up()
 
     @pl.when(stage > 0)
@@ -455,57 +489,113 @@
             x_side.arrive(me, c)
         own_up(True)
 
-    def spread_in(side, step, pieces_of, add, group):
-        @pl.loop(0, side.pieces // group)
-        def _(j):
-            for g in range(group):
-                c = j * group + g
-                side.relay(step, c)
-
-                @pl.when(c < side.pieces - 1)
-                def _():
-                    side.arrive(shard(step - 1, True), c)
-
-                @pl.when(c == side.pieces - 1)
-                def _():
-                    side.relay_extra(step - 1)
-
-            add([(t, j * group + g) for t in pieces_of for g in range(group)])
-
-    for i in range(1, depth):
-        fresh = [shard(i - 1, True), shard(i, False)]
-
-        @pl.when(stage == 0)
-        def _():
-            for t in fresh:
-                up_copy(t).wait()
-            if i == 1:
-                start_tables(tables[1])
-            if i == 2:
-                start_each(up_copy, visits[6:])
-            if i == depth - 1:
-                start_each(down_copy, visits[:3])
-
-        spread_in(x_side, i, fresh, lambda items: per_stage(functools.partial(up_add, items, False)), 2 if x_pieces % 2 == 0 else 1)
-        if i == 1:
-            @pl.when(stage == 0)
+    def first_relay(side, c):
+        side.relay(1, c)
+
+        @pl.when(c < side.pieces - 1)
+        def _():
+            side.arrive(partner, c)
+
+        @pl.when(c == side.pieces - 1)
+        def _():
+            side.relay_extra(0)
+
+    def second_relay(side, c):
+        side.relay(2, c)
+
+        @pl.when(jnp.logical_and(c < side.pieces - 1, jnp.logical_not(inner)))
+        def _():
+            side.arrive(near_other, c)
+
+        @pl.when(c == side.pieces - 1)
+        def _():
+            side.relay_extra(1)
+
+    def third_relay(side, c, full):
+        side.relay(3, c)
+        if full:
+            @pl.when(inner)
             def _():
-                start_each(up_copy, visits[3:6])
-                panels(tables[1], expand)
-
-            @pl.when(stage > 0)
+                side.arrive(near_other, c)
+
+            side.arrive(second_other, c)
+        else:
+            @pl.when(inner)
             def _():
-                send_part()
-
-    last = shard(depth - 1, True)
+                side.relay_extra(2)
+
+    def end_extras(side):
+        @pl.when(jnp.logical_not(inner))
+        def _():
+            side.relay_extra(2)
+
+        side.relay_extra(3)
+
+    def up_more(*items):
+        per_stage(functools.partial(up_add, list(items), False))
 
     @pl.when(stage == 0)
     def _():
+        for t in (partner, shard(1, False)):
+            up_copy(t).wait()
+        start_each(up_copy, visits[5:])
+
+    pair = 2
+    end = x_pieces - 1
+
+    @pl.loop(0, x_pieces // pair)
+    def _(j):
+        for c in (pair * j, pair * j + 1):
+            first_relay(x_side, c)
+        up_more(*[(t, pair * j + g) for t in (partner, shard(1, False)) for g in range(pair)])
+
+    @pl.when(stage > 0)
+    def _():
+        send_part()
+
+    @pl.when(stage == 0)
+    def _():
+        start_expand()
+        for t in visits[3:5]:
+            up_copy(t).wait()
+
+        @pl.when(inner)
+        def _():
+            up_copy(shard(3, False)).wait()
+
+    @pl.loop(0, x_pieces // pair)
+    def _(j):
+        for c in (pair * j, pair * j + 1):
+            second_relay(x_side, c)
+        up_more(*[(t, pair * j + g) for t in (second_turn, shard(2, False)) for g in range(pair)])
+
+    @pl.when(stage == 0)
+    def _():
+        start_each(down_copy, down_early)
+        up_copy(second_other).wait()
+
+        @pl.when(jnp.logical_not(inner))
+        def _():
+            up_copy(shard(3, False)).wait()
+
+    for c in range(0, x_pieces - pair, pair):
+        for g in range(pair):
+            third_relay(x_side, c + g, True)
+        up_more(*[(t, c + g) for t in (third_turn, second_other) for g in range(pair)])
+    third_relay(x_side, end - 1, True)
+    third_relay(x_side, end, False)
+
+    @pl.when(stage == 0)
+    def _():
         up_copy(last).wait()
 
-    for c in range(x_pieces - 2):
+    for c in range(end - 2):
         x_side.arrive(last, c)
-    per_stage(functools.partial(up_add, [(last, c) for c in range(x_pieces - 2)], False))
+    up_more((third_turn, end - 1), (third_turn, end), (second_other, end - 1), *[(last, c) for c in range(end - 2)])
+
+    x_side.arrive(last, end - 2)
+    end_extras(x_side)
+    up_more((last, end - 2), (second_other, end), (last, end))
 
     others = partial.at[0:shards - 1]
     all_parts = pltpu.make_async_remote_copy(
@@ -521,11 +611,10 @@
 
     @pl.when(stage == 0)
     def _():
-        start_each(down_copy, visits[3:5])
-
-    x_side.arrive(last, x_pieces - 2)
-    x_side.relay_extra(depth - 1)
-    finals = [(last, x_pieces - 2), (last, x_pieces - 1)]
+        expand_panel(0)
+
+    x_side.arrive(last, end - 1)
+    finals = [(last, end - 1)]
     square = sq[...]
     lefts = []
     for t, c in finals:
@@ -535,16 +624,22 @@
     inverse = lax.rsqrt(jnp.sum(square, axis=1, keepdims=True) / width + EPSILON)
     low_rank = (low * inverse).astype(bf16)
 
+    lag = 4
+
     def up_finish(flipped):
         for n in range(a_pieces):
             block = slice(n * PIECE, (n + 1) * PIECE)
             base = jnp.zeros((rows, PIECE), f32)
             for (t, c), left in zip(finals, lefts):
                 base += up_dot(left, n, t, c, flipped)
+            if n and not flipped:
+                expand_panel(n)
             adapted = lax.dot_general(low_rank, expand[block, :], NT, preferred_element_type=f32)
             value = inverse * (acc[:, block] + base) + adapted
             act[me, n] = (value / (1.0 + jnp.exp(-value))).astype(bf16)
             a_side.start_own(n)
+            if n >= lag and not flipped:
+                first_relay(a_side, jnp.int32(n - lag))
 
     per_stage(up_finish)
 
@@ -562,24 +657,56 @@
 
     @pl.when(stage == 0)
     def _():
-        start_each(down_copy, visits[5:])
+        start_each(down_copy, down_late)
 
     for n in range(x_pieces):
         acc[:, n * PIECE:(n + 1) * PIECE] = xs[me, n].astype(f32)
 
-    down_copy(me).wait()
-    for i in range(1, depth):
-        fresh = [shard(i - 1, True), shard(i, False)]
-        for t in fresh:
-            down_copy(t).wait()
-        spread_in(a_side, i, ([me] if i == 1 else []) + fresh, down_add, 1)
-
-    down_copy(last).wait()
-
-    @pl.loop(0, a_pieces - 2)
+    for t in down_early[:3]:
+        down_copy(t).wait()
+    end = a_pieces - 1
+
+    @pl.loop(0, a_pieces)
     def _(c):
+        @pl.when(jnp.logical_or(stage > 0, c >= a_pieces - lag))
+        def _():
+            first_relay(a_side, c)
+
+        down_add([(me, c), (partner, c), (shard(1, False), c)])
+
+    for t in down_early[3:]:
+        down_copy(t).wait()
+
+    @pl.loop(0, a_pieces)
+    def _(c):
+        second_relay(a_side, c)
+        down_add([(second_turn, c), (shard(2, False), c)])
+
+    for t in down_late:
+        down_copy(t).wait()
+
+    late = max(end - 2, 0)
+
+    @pl.loop(0, late)
+    def _(c):
+        third_relay(a_side, c, True)
+        down_add([(third_turn, c), (second_other, c)])
+
+    @pl.loop(late, end)
+    def _(c):
+        third_relay(a_side, c, True)
+        a_side.arrive(last, c - late)
+        down_add([(third_turn, c), (second_other, c), (last, c - late)])
+
+    third_relay(a_side, end, False)
+    a_side.arrive(last, end - late)
+    down_add([(third_turn, end), (last, end - late)])
+    rest = list(range(end - late + 1, end - 1))
+    for c in rest:
         a_side.arrive(last, c)
-        down_add([(last, c)])
+    down_add([(last, c) for c in rest])
+    end_extras(a_side)
+    down_add([(second_other, end), (last, end)])
 
     row = lax.broadcasted_iota(jnp.int32, (rows, 1), 0)
     kept = row < 0
@@ -587,13 +714,11 @@
         start = s * seg_rows
         kept = jnp.logical_or(kept, jnp.logical_and(row >= start, row < start + jnp.minimum(live_ref[s], seg_rows)))
 
-    a_side.arrive(last, a_pieces - 2)
-    a_side.relay_extra(depth - 1)
+    a_side.arrive(last, end - 1)
     for n in range(x_pieces):
         block = slice(n * PIECE, (n + 1) * PIECE)
         part = jnp.zeros((rows, PIECE), f32)
-        for c in (a_pieces - 2, a_pieces - 1):
-            part += lax.dot_general(act[last, c], down_tile(n, last, c), NT, preferred_element_type=f32)
+        part += lax.dot_general(act[last, end - 1], down_tile(n, last, end - 1), NT, preferred_element_type=f32)
         out_v[n] = jnp.where(kept, acc[:, block] + part, 0.0).astype(bf16)
         hand_each(n)
         out_copy(n).start()
@@ -616,7 +741,7 @@
     hbm = pl.BlockSpec(memory_space=pl.ANY)
     dma = pltpu.SemaphoreType.DMA
     flat = PIECE * rank
-    blocks = table_blocks(shards * hidden // flat * flat, shrink_weight, expand_weight)
+    blocks = table_blocks(shards * hidden // flat * flat, shrink_weight) + a_pieces
     return pl.pallas_call(
         section_kernel,
         out_shape=jax.ShapeDtypeStruct((rows, cols), jnp.bfloat16),
@@ -655,13 +780,18 @@
     rank = flat_cols // col_count
     flat = PIECE * rank
     width = shards * hidden // flat * flat
-    if col_count % PIECE or hidden % PIECE or hidden < 4 * PIECE or col_count < 4 * PIECE:
+    if col_count % PIECE or hidden % PIECE or hidden < 5 * PIECE or col_count // PIECE != 4:
         return False
     if row_count > LANES or rank * 8 != LANES or segments * rank > LANES or adapters % LANES:
         return False
-    if shards % COLUMNS or shards < 2 * COLUMNS or col_count > hidden:
+    if shards != 4 * COLUMNS or col_count > hidden:
         return False
-    if not width or table_blocks(width, shrink_weight, expand_weight) * adapters > col_count:
+    if not width or hidden % LANES:
+        return False
+    whole, rest = flat // hidden, flat % hidden
+    spots = 3 * (col_count // adapters - table_blocks(width, shrink_weight))
+    pieces = hidden // PIECE
+    if pieces * whole + (-(-pieces // (hidden // rest)) if rest else 0) > spots:
         return False
     return 2 * hidden * col_count * 2 * shards < VMEM_BYTES - 7 * 2**20
 

time: 84.4 us -> 84 us (level)
  no operation moved by 1% of the time
where the time goes in v4:
time: 84 us; the launch traced here: 83.8 us
  Pallas kernels  82.1 us (98%)
  local copies, waits for them, and re-layouts  1.65 us (2%)
    pallas_call x1, Pallas kernels, fused_sections(): pl.pallas_call(section_kernel, out_shape=jax.ShapeDtypeStruct((rows, cols...  82.1 us

profile of v4, /device:TPU:1, one launch (start us, length us, event | category | flops | bytes accessed | tf_op | source)
XLA Modules:
  0.0 83.8 jit_solution(871974860427854419)
XLA Ops:
  0.0 82.1 %shard_map.82 = bf16[120,1024]{1,0:T(8,128)(2,1)} custom-call(s32[3]{0:T(128)} %bitcast.14, s32[3]{0:T(128)} %bitcast.15, f32[1,8192]{1,0:T(1,128)} %gain_ref.1, bf16[120,1024]{1,0:T(8,128)(2,1)} %bitcast.13, bf16[128,16384]{1,0:T(8,128)(2,1)} %bitcast.11, bf16[128,28672]{1,0:T(8,128)(2,1)} %bitcast.10, bf16[1792,8192]{1,0:T(8,128)(2,1)} %bitcast.8, ...), custom_call_target="tpu_custom_call" | custom-call | tf_op jit(solution)/shard_map/pallas_call | solution.py:745
  82.2 1.7 %copy.10 = bf16[1,1,120,1024]{3,2,1,0:T(8,128)(2,1)} copy(bf16[1,1,120,1024]{3,2,1,0:T(8,128)(2,1)} %bitcast.12) | data formatting | bytes 491520

commit v5 on v4

--- a/solution.py
+++ b/solution.py
@@ -359,7 +359,7 @@
     def shrink_panels(then):
         for k, size, copy in shrink_blocks:
             copy.wait()
-        start_each(up_copy, then)
+        then()
         done = 0
         for k, size, copy in shrink_blocks:
             first = done
@@ -472,12 +472,12 @@
     def _():
         for c in range(x_pieces):
             x_side.start_own(c)
-        shrink_panels(visits[3:5])
+        shrink_panels(lambda: start_each(up_copy, visits[3:5] + visits[6:7]))
         send_part()
 
     @pl.when(stage > 0)
     def _():
-        shrink_panels([])
+        shrink_panels(lambda: None)
         for n in range(a_pieces):
             expand_panel(n)
         start_each(down_copy, down_early + down_late)
@@ -538,7 +538,7 @@
     def _():
         for t in (partner, shard(1, False)):
             up_copy(t).wait()
-        start_each(up_copy, visits[5:])
+        start_expand()
 
     pair = 2
     end = x_pieces - 1
@@ -555,7 +555,9 @@
 
     @pl.when(stage == 0)
     def _():
-        start_expand()
+        start_each(up_copy, visits[5:6] + visits[7:])
+        for n in range(3):
+            expand_panel(n)
         for t in visits[3:5]:
             up_copy(t).wait()
 
@@ -572,6 +574,8 @@
     @pl.when(stage == 0)
     def _():
         start_each(down_copy, down_early)
+        for n in range(3, a_pieces - 2):
+            expand_panel(n)
         up_copy(second_other).wait()
 
         @pl.when(jnp.logical_not(inner))
@@ -608,10 +612,6 @@
         summed = summed + partial[t]
     stacked = jnp.concatenate([summed] * segments + [jnp.zeros((LANES - segments * rank, LANES), f32)], axis=0)
     low = jnp.where(in_segment, jnp.transpose(stacked)[:rows], 0.0)
-
-    @pl.when(stage == 0)
-    def _():
-        expand_panel(0)
 
     x_side.arrive(last, end - 1)
     finals = [(last, end - 1)]
@@ -624,22 +624,19 @@
     inverse = lax.rsqrt(jnp.sum(square, axis=1, keepdims=True) / width + EPSILON)
     low_rank = (low * inverse).astype(bf16)
 
-    lag = 4
-
     def up_finish(flipped):
         for n in range(a_pieces):
             block = slice(n * PIECE, (n + 1) * PIECE)
             base = jnp.zeros((rows, PIECE), f32)
             for (t, c), left in zip(finals, lefts):
                 base += up_dot(left, n, t, c, flipped)
-            if n and not flipped:
-                expand_panel(n)
             adapted = lax.dot_general(low_rank, expand[block, :], NT, preferred_element_type=f32)
             value = inverse * (acc[:, block] + base) + adapted
             act[me, n] = (value / (1.0 + jnp.exp(-value))).astype(bf16)
             a_side.start_own(n)
-            if n >= lag and not flipped:
-                first_relay(a_side, jnp.int32(n - lag))
+            ready = a_pieces - 4 + n
+            if n > 1 and a_pieces - 2 <= ready < a_pieces and not flipped:
+                expand_panel(ready)
 
     per_stage(up_finish)
 
@@ -668,10 +665,7 @@
 
     @pl.loop(0, a_pieces)
     def _(c):
-        @pl.when(jnp.logical_or(stage > 0, c >= a_pieces - lag))
-        def _():
-            first_relay(a_side, c)
-
+        first_relay(a_side, c)
         down_add([(me, c), (partner, c), (shard(1, False), c)])
 
     for t in down_early[3:]:
@@ -780,7 +774,7 @@
     rank = flat_cols // col_count
     flat = PIECE * rank
     width = shards * hidden // flat * flat
-    if col_count % PIECE or hidden % PIECE or hidden < 5 * PIECE or col_count // PIECE != 4:
+    if col_count % PIECE or hidden % PIECE or hidden < 7 * PIECE or col_count // PIECE != 4:
         return False
     if row_count > LANES or rank * 8 != LANES or segments * rank > LANES or adapters % LANES:
         return False

time: 84 us -> 83.1 us (0.989)
  Pallas kernels: 82.1 us -> 81.2 us
    pallas_call x1, Pallas kernels: 82.1 us -> 81.2 us  [fused_sections(): pl.pallas_call(section_kernel, out_shape=jax.ShapeDtypeStruct((rows, cols...]
where the time goes in v5:
time: 83.1 us; the launch traced here: 82.8 us
  Pallas kernels  81.2 us (98%)
  local copies, waits for them, and re-layouts  1.65 us (2%)
    pallas_call x1, Pallas kernels, fused_sections(): pl.pallas_call(section_kernel, out_shape=jax.ShapeDtypeStruct((rows, cols...  81.2 us

profile of v5, /device:TPU:1, one launch (start us, length us, event | category | flops | bytes accessed | tf_op | source)
XLA Modules:
  0.0 82.8 jit_solution(16297753143771275517)
XLA Ops:
  0.0 81.2 %shard_map.82 = bf16[120,1024]{1,0:T(8,128)(2,1)} custom-call(s32[3]{0:T(128)} %bitcast.14, s32[3]{0:T(128)} %bitcast.15, f32[1,8192]{1,0:T(1,128)} %gain_ref.1, bf16[120,1024]{1,0:T(8,128)(2,1)} %bitcast.13, bf16[128,16384]{1,0:T(8,128)(2,1)} %bitcast.11, bf16[128,28672]{1,0:T(8,128)(2,1)} %bitcast.10, bf16[1792,8192]{1,0:T(8,128)(2,1)} %bitcast.8, ...), custom_call_target="tpu_custom_call" | custom-call | tf_op jit(solution)/shard_map/pallas_call | solution.py:739
  81.2 1.7 %copy.10 = bf16[1,1,120,1024]{3,2,1,0:T(8,128)(2,1)} copy(bf16[1,1,120,1024]{3,2,1,0:T(8,128)(2,1)} %bitcast.12) | data formatting | bytes 491520
